TPU v7x, 32 devices: a whole 2x2x4 slice. The times are simulated.
32 devices in a mesh: groups: 2 (over x), expert: 16 (over z, y, core).
Axes of the slice: x: 2, y: 2, z: 4, core: 2. Of those that a mesh axis runs over, the one named last changes fastest.
Arguments:
- tokens: bfloat16 [4096, 7168], P(('groups', 'expert')), parts along dimension 0, may hold values from -6 to 6
- route_ids: int32 [4096, 2], P(('groups', 'expert')), parts along dimension 0, may hold values from 0 to 3, all different within a row; in each aligned block of 128 rows (0 to 127, 128 to 255, ...) at most 80 rows name the same one
- levels: int32 [4096, 2], P(('groups', 'expert')), parts along dimension 0, may hold values from 1 to 64
- w_gate: bfloat16 [16, 7168, 512], P('expert'), may hold values from -0.0625 to 0.0625
- w_up: bfloat16 [16, 7168, 512], P('expert'), may hold values from -0.0625 to 0.0625
- w_down: bfloat16 [16, 512, 7168], P('expert'), may hold values from -0.125 to 0.125
Outputs:
- combined: bfloat16 [4096, 7168], P(('groups', 'expert')), parts along dimension 0
There are 2 independent parts, one for each index of `groups`. A program takes and returns all parts, laid end to end along the dimension named above; an argument that names none is the same for every part. Nothing has to cross between parts.
Inputs may be any that keep to these rules, and one draw needn't show every extreme that they name: `route_ids`: each row names 2 different experts; among the rows of one device no expert is named more than 80 times, a bound that some block reaches.
All inputs are finite; a program needn't handle non-finite values.
Results may differ from a plain program's by a relative error of at most 0.013.
Values may be sent and summed in bfloat16 or wider, within the bound.
A program may use at most 192 MiB of HBM per device.

v0:
```python
import functools

import jax
import jax.numpy as jnp
from jax import lax
from jax.experimental import pallas as pl
from jax.experimental.pallas import tpu as pltpu
from jax.sharding import PartitionSpec as P

SHARDS = 4
MESH = pl.DeviceIdType.MESH


def tile_of(length, most):
    size = most
    while length % size:
        size //= 2
    return size


def xor(a, mask, count):
    total, bit = 0, 1
    while bit < count:
        total += (a // bit + mask // bit) % 2 * bit
        bit *= 2
    return total


def layer_kernel(
    planes, out_ref, gate_hbm, up_hbm, down_hbm, ret_ref,
    x, gate, up, down, acc, hidden, pair, cross,
    w_sem, z_send, z_recv, y_send, y_recv, p_send, p_recv,
    rp_send, rp_recv, ry_send, ry_recv, rz_send, rz_recv,
):
    me = lax.axis_index("expert")
    plane, s = me // SHARDS, me % SHARDS
    base = plane * SHARDS
    core, row = s % 2, s // 2
    partner_s = row * 2 + (1 - core)
    cross_s = (1 - row) * 2 + core
    diag_s = (1 - row) * 2 + (1 - core)
    partner, neighbour = base + partner_s, base + cross_s
    cap, width = x.shape[2], x.shape[3]
    rows = SHARDS * cap
    tile = tile_of(width, 1024)
    chunks = width // tile

    barrier = pltpu.get_barrier_semaphore()
    peers = [partner, neighbour]
    peers += [xor(plane, j, planes) * SHARDS + s for j in range(1, planes)]
    for peer in peers:
        pl.semaphore_signal(barrier, inc=1, device_id={"expert": peer}, device_id_type=MESH)
    pl.semaphore_wait(barrier, planes + 1)

    def remote(src, dst, send, recv, device):
        return pltpu.make_async_remote_copy(
            src_ref=src, dst_ref=dst, send_sem=send, recv_sem=recv,
            device_id={"expert": device}, device_id_type=MESH,
        )

    def columns(q):
        return pl.ds(pl.multiple_of(q * tile, tile), tile)

    def out_copy(j):
        to = xor(plane, j, planes)
        return remote(out_ref.at[to], x.at[j, s], z_send.at[j], z_recv.at[j], to * SHARDS + s)

    def own_copy():
        return pltpu.make_async_copy(out_ref.at[plane], x.at[0, s], z_recv.at[0])

    def y_copy(j):
        return remote(x.at[j, s], x.at[j, s], y_send.at[j], y_recv.at[j], neighbour)

    def y_arrival(j):
        return remote(x.at[j, cross_s], x.at[j, cross_s], y_send.at[j], y_recv.at[j], neighbour)

    def p_copy(j, k, slot):
        return remote(x.at[j, slot], x.at[j, slot], p_send.at[j, k], p_recv.at[j, k], partner)

    def rp_copy(j, q, k, slot):
        cols = columns(q)
        return remote(
            x.at[j, slot, :, cols], pair.at[j, k, :, cols],
            rp_send.at[j, q, k], rp_recv.at[j, q, k], partner,
        )

    def ry_copy(j, q):
        cols = columns(q)
        return remote(
            x.at[j, cross_s, :, cols], cross.at[j, :, cols],
            ry_send.at[j, q], ry_recv.at[j, q], neighbour,
        )

    def rz_copy(j, q):
        cols, to = columns(q), xor(plane, j, planes)
        return remote(
            x.at[j, s, :, cols], ret_ref.at[plane, :, cols],
            rz_send.at[j, q], rz_recv.at[j, q], to * SHARDS + s,
        )

    def keep_copy(q):
        cols = columns(q)
        return pltpu.make_async_copy(x.at[0, s, :, cols], ret_ref.at[plane, :, cols], rz_send.at[0, q])

    own_copy().start()
    for distance in range(1, planes):
        for to in (plane + distance, plane - distance):
            @pl.when((to >= 0) & (to < planes))
            def _():
                mask = xor(plane, to, planes)
                remote(
                    out_ref.at[to], x.at[mask, s], z_send.at[mask], z_recv.at[mask], to * SHARDS + s
                ).start()
    loads = [
        pltpu.make_async_copy(gate_hbm.at[0], gate, w_sem.at[0]),
        pltpu.make_async_copy(up_hbm.at[0], up, w_sem.at[1]),
        pltpu.make_async_copy(down_hbm.at[0], down, w_sem.at[2]),
    ]
    for load in loads:
        load.start()

    def arrive(j):
        if j == 0:
            own_copy().wait()
        else:
            out_copy(j).wait_recv()
        y_copy(j).start()
        p_copy(j, 0, s).start()

    def gather(j):
        y_arrival(j).wait_recv()
        p_copy(j, 1, cross_s).start()
        p_copy(j, 0, partner_s).wait_recv()
        p_copy(j, 1, diag_s).wait_recv()

    def expand(j):
        @pl.loop(0, chunks)
        def _(q):
            cols = columns(q)
            part = x[j, :, :, cols].reshape(rows, tile)

            @pl.when(q == 0)
            def _():
                acc[...] = jnp.zeros_like(acc)

            acc[0] += jnp.dot(part, gate[cols, :], preferred_element_type=jnp.float32)
            acc[1] += jnp.dot(part, up[cols, :], preferred_element_type=jnp.float32)

        value = acc[0]
        hidden[...] = (value / (1.0 + jnp.exp(-value)) * acc[1]).astype(hidden.dtype)

    def contract(j):
        y_copy(j).wait_send()
        p_copy(j, 0, s).wait_send()
        p_copy(j, 1, cross_s).wait_send()

        @pl.loop(0, chunks + 1)
        def _(q):
            @pl.when(q < chunks)
            def _():
                cols = columns(q)
                part = jnp.dot(hidden[...], down[:, cols], preferred_element_type=jnp.float32)
                x[j, :, :, cols] = part.astype(x.dtype).reshape(SHARDS, cap, tile)
                rp_copy(j, q, 1 - row, diag_s).start()
                rp_copy(j, q, row, partner_s).start()

            @pl.when(q > 0)
            def _():
                cols = columns(q - 1)
                rp_copy(j, q - 1, 1 - row, diag_s).wait_recv()
                total = x[j, cross_s, :, cols].astype(jnp.float32)
                total += pair[j, 1 - row, :, cols].astype(jnp.float32)
                x[j, cross_s, :, cols] = total.astype(x.dtype)
                ry_copy(j, q - 1).start()

    def finish(j):
        @pl.loop(0, chunks)
        def _(q):
            cols = columns(q)
            rp_copy(j, q, row, partner_s).wait_recv()
            total = x[j, s, :, cols].astype(jnp.float32) + pair[j, row, :, cols].astype(jnp.float32)
            ry_copy(j, q).wait_recv()
            x[j, s, :, cols] = (total + cross[j, :, cols].astype(jnp.float32)).astype(x.dtype)
            if j > 0:
                rz_copy(j, q).start()
            else:
                keep_copy(q).start()

    order = [0, *range(2, planes), 1]
    arrive(0)
    arrive(1)
    for i, j in enumerate(order):
        gather(j)
        if 0 < i < planes - 2:
            arrive(order[i + 1])
        if i == 0:
            for load in loads:
                load.wait()
        expand(j)
        contract(j)
        if i == 0:
            arrive(order[1])
        else:
            finish(order[i - 1])
    finish(order[-1])

    for j in range(planes):
        @pl.loop(0, chunks)
        def _(q):
            rp_copy(j, q, 1 - row, diag_s).wait_send()
            rp_copy(j, q, row, partner_s).wait_send()
            ry_copy(j, q).wait_send()
            if j > 0:
                rz_copy(j, q).wait()
            else:
                keep_copy(q).wait()
        if j > 0:
            out_copy(j).wait_send()


def combine_kernel(weight_ref, ret_ref, out_ref):
    weight = weight_ref[...]
    high = weight.astype(jnp.bfloat16)
    low = (weight - high.astype(jnp.float32)).astype(jnp.bfloat16)
    total = jnp.dot(high, ret_ref[...], preferred_element_type=jnp.float32)
    total += jnp.dot(low, ret_ref[...], preferred_element_type=jnp.float32)
    out_ref[...] = total.astype(out_ref.dtype)


def on_device(tokens, route_ids, levels, w_gate, w_up, w_down):
    tok_rows, width = tokens.shape
    top = route_ids.shape[1]
    ff = w_gate.shape[2]
    experts = lax.axis_size("expert") // SHARDS
    capacity = 5 * tok_rows * top // (4 * experts)
    cap = -(-capacity // 16) * 16
    slots = experts * cap
    dtype = tokens.dtype

    chosen = route_ids[:, :, None] == jnp.arange(experts, dtype=jnp.int32)
    named = jnp.any(chosen, axis=1)
    index = jnp.arange(tok_rows, dtype=jnp.int32)
    earlier = (index[:, None] > index[None, :]).astype(jnp.bfloat16)
    rank = jnp.dot(earlier, named.astype(jnp.bfloat16), preferred_element_type=jnp.float32)
    place = jnp.where(named, rank.astype(jnp.int32), cap)
    level_f = levels.astype(jnp.float32)
    weights = level_f / jnp.sum(level_f, axis=1, keepdims=True)
    weight_e = jnp.sum(jnp.where(chosen, weights[:, :, None], 0.0), axis=1)
    spot = jnp.arange(cap, dtype=jnp.int32)
    pick = (place[:, :, None] == spot).reshape(tok_rows, slots)
    weight_m = jnp.where(pick, jnp.repeat(weight_e, cap, axis=1), 0.0)
    outgoing = lax.dot_general(
        pick.astype(dtype), tokens, (((0,), (0,)), ((), ())), preferred_element_type=jnp.float32
    ).astype(dtype).reshape(experts, cap, width)

    dma, anywhere = pltpu.SemaphoreType.DMA, pl.BlockSpec(memory_space=pl.ANY)
    rows, chunks = SHARDS * cap, width // tile_of(width, 1024)
    returned = pl.pallas_call(
        functools.partial(layer_kernel, experts),
        out_shape=jax.ShapeDtypeStruct((experts, cap, width), dtype),
        in_specs=[anywhere] * 4,
        out_specs=anywhere,
        scratch_shapes=[
            pltpu.VMEM((experts, SHARDS, cap, width), dtype),
            pltpu.VMEM((width, ff), dtype),
            pltpu.VMEM((width, ff), dtype),
            pltpu.VMEM((ff, width), dtype),
            pltpu.VMEM((2, rows, ff), jnp.float32),
            pltpu.VMEM((rows, ff), dtype),
            pltpu.VMEM((experts, 2, cap, width), dtype),
            pltpu.VMEM((experts, cap, width), dtype),
            dma((3,)),
            dma((experts,)), dma((experts,)),
            dma((experts,)), dma((experts,)),
            dma((experts, 2)), dma((experts, 2)),
            dma((experts, chunks, 2)), dma((experts, chunks, 2)),
            dma((experts, chunks)), dma((experts, chunks)),
            dma((experts, chunks)), dma((experts, chunks)),
        ],
        compiler_params=pltpu.CompilerParams(
            collective_id=0, has_side_effects=True, vmem_limit_bytes=67_000_000
        ),
    )(outgoing, w_gate, w_up, w_down)

    tile = tile_of(width, 1024)
    return pl.pallas_call(
        combine_kernel,
        out_shape=jax.ShapeDtypeStruct((tok_rows, width), dtype),
        grid=(width // tile,),
        in_specs=[
            pl.BlockSpec((tok_rows, slots), lambda n: (0, 0)),
            pl.BlockSpec((slots, tile), lambda n: (0, n)),
        ],
        out_specs=pl.BlockSpec((tok_rows, tile), lambda n: (0, n)),
    )(weight_m, returned.reshape(slots, width))


def solution(mesh):
    return jax.shard_map(
        on_device,
        mesh=mesh,
        in_specs=(
            P(("groups", "expert"), None),
            P(("groups", "expert"), None),
            P(("groups", "expert"), None),
            P("expert", None, None),
            P("expert", None, None),
            P("expert", None, None),
        ),
        out_specs=P(("groups", "expert"), None),
        check_vma=False,
    )
```

profile of v0, /device:TPU:0, one launch (start us, length us, event | category | flops | bytes accessed | tf_op | source)
XLA Modules:
  0.0 267.8 jit_solution(6302047924982540394)
XLA Ops:
  0.0 0.7 fusion.1
  0.7 0.7 convert_reduce_fusion
  1.4 0.7 convert_divide_fusion
  2.1 0.7 select_reduce_fusion
  2.8 0.1 fusion
  2.9 0.1 eq.39
  3.0 0.1 copy.14
  3.2 0.1 copy.15
  3.3 0.7 broadcast_select_fusion
  4.0 5.0 %convolution_convert_fusion = bf16[320,7168]{1,0:T(8,128)(2,1)} fusion(pred[128,320]{1,0:T(32,128)(4,1)S(1)} %get-tuple-element.6, bf16[128,7168]{1,0:T(8,128)(2,1)} %param.6), kind=kOutput, calls=%fused_computation | convolution fusion | flops 589496320 | bytes 6463488 | tf_op jit(solution)/shard_map/dot_general | solution.py:252
  9.1 251.4 %shard_map.64 = bf16[4,80,7168]{2,1,0:T(8,128)(2,1)} custom-call(bf16[4,80,7168]{2,1,0:T(8,128)(2,1)} %bitcast.7, bf16[1,7168,512]{2,1,0:T(8,128)(2,1)} %gate_hbm.1, bf16[1,7168,512]{2,1,0:T(8,128)(2,1)} %up_hbm.1, bf16[1,512,7168]{2,1,0:T(8,128)(2,1)} %down_hbm.1), custom_call_target="tpu_custom_call" | custom-call | tf_op jit(solution)/shard_map/pallas_call | solution.py:258
  260.5 7.3 %shard_map.65 = bf16[128,7168]{1,0:T(8,128)(2,1)} custom-call(f32[128,320]{1,0:T(8,128)} %get-tuple-element.5.weight_ref, bf16[320,7168]{1,0:T(8,128)(2,1)} %bitcast.8), custom_call_target="tpu_custom_call" | custom-call | tf_op jit(solution)/shard_map/pallas_call | solution.py:286
  (3 shorter events, 0.0 us)
where the time goes:
time: 268 us
  Pallas kernels  259 us (97%)
  matrix products  5.18 us (2%)
  other arithmetic  3.5 us (1%)
    pallas_call x1, Pallas kernels, on_device(): pl.pallas_call(functools.partial(layer_kernel, experts), out_shape=jax.Sh...  251 us
    pallas_call x1, Pallas kernels, on_device(): pl.pallas_call(combine_kernel, out_shape=jax.ShapeDtypeStruct((tok_rows,...  7.29 us

commit v1 on v0

--- a/solution.py
+++ b/solution.py
@@ -218,6 +218,470 @@
             out_copy(j).wait_send()
 
 
+def routed_kernel(
+    tokens, ids, levels, gate_hbm, up_hbm, down_hbm, out_hbm,
+    x, gate, up, down, acc, hidden, pair, cross, raw, raw_y, raw_f,
+    near_stage, far_stage, near_ret, outer_ret, far_ret, table, picks, mix,
+    w_sem, raw_sem, out_sem, table_send, table_recv,
+    cross_send, cross_recv, far_send, far_recv, near_send, near_recv,
+    fwd_send, fwd_recv, y_send, y_recv, d_send, d_recv,
+    rp_send, rp_recv, ry_send, ry_recv,
+    nr_send, nr_recv, or_send, or_recv, fr_send, fr_recv,
+    pair_free, cross_free,
+):
+    me = lax.axis_index("expert")
+    plane, s = me // SHARDS, me % SHARDS
+    core, row = s % 2, s // 2
+    half, near_plane = plane // 2, xor(plane, 1, 4)
+    far_plane = 2 * (1 - half) + half
+    kind = (plane + half + 1) % 2
+    inner, outer = kind == 0, kind == 1
+    cross_s = (1 - row) * 2 + core
+    partner_s = row * 2 + (1 - core)
+    diag_s = (1 - row) * 2 + (1 - core)
+    partner, neighbour = plane * SHARDS + partner_s, plane * SHARDS + cross_s
+    near, far = near_plane * SHARDS + s, far_plane * SHARDS + s
+    far_b = xor(far_plane, 1, 4) * SHARDS + s
+    cap, width = x.shape[2], x.shape[3]
+    tok_rows = raw.shape[0]
+    rows = SHARDS * cap
+    tile = tile_of(width, 1024)
+    chunks = width // tile
+    own_j, near_j = 0, 1
+
+    def columns(q):
+        return pl.ds(pl.multiple_of(q * tile, tile), tile)
+
+    def remote(src, dst, send, recv, device):
+        return pltpu.make_async_remote_copy(
+            src_ref=src, dst_ref=dst, send_sem=send, recv_sem=recv,
+            device_id={"expert": device}, device_id_type=MESH,
+        )
+
+    def each(body):
+        pl.loop(0, chunks)(body)
+
+    raw_load = pltpu.make_async_copy(tokens, raw, raw_sem)
+    loads = [
+        pltpu.make_async_copy(gate_hbm.at[0], gate, w_sem.at[0]),
+        pltpu.make_async_copy(up_hbm.at[0], up, w_sem.at[1]),
+        pltpu.make_async_copy(down_hbm.at[0], down, w_sem.at[2]),
+    ]
+    raw_load.start()
+
+    barrier = pltpu.get_barrier_semaphore()
+    peers = [partner, neighbour, near, far, far_b]
+    for peer in peers:
+        pl.semaphore_signal(barrier, inc=1, device_id={"expert": peer}, device_id_type=MESH)
+
+    lane = lax.broadcasted_iota(jnp.int32, (tok_rows, tok_rows), 1)
+    line = lax.broadcasted_iota(jnp.int32, (tok_rows, tok_rows), 0)
+    first, second = ids[:, 0:1] == lane, ids[:, 1:2] == lane
+    level_0, level_1 = levels[:, 0:1].astype(jnp.float32), levels[:, 1:2].astype(jnp.float32)
+    named = jnp.where(first | second, 1.0, 0.0)
+    earlier = jnp.where(line > lane, 1.0, 0.0).astype(jnp.bfloat16)
+    rank = jnp.dot(earlier, named.astype(jnp.bfloat16), preferred_element_type=jnp.float32)
+    place = jnp.where(named > 0.0, rank, 2.0 * tok_rows)
+    share = jnp.where(first, level_0 / (level_0 + level_1), 0.0)
+    share += jnp.where(second, level_1 / (level_0 + level_1), 0.0)
+    table[0, 0:8, :] = jnp.transpose(place)[0:8, :]
+    table[0, 8:16, :] = jnp.transpose(share)[0:8, :]
+
+    def matches(k, expert):
+        spot = lax.broadcasted_iota(jnp.int32, (cap, tok_rows), 0).astype(jnp.float32)
+        return table[k, pl.ds(expert, 1), :] == spot
+
+    def set_pick(k):
+        for i, expert in enumerate((plane, near_plane)):
+            pick = jnp.where(matches(k, expert), 1.0, 0.0)
+            picks[k, i * cap:(i + 1) * cap, :] = pick.astype(picks.dtype)
+
+    def set_mix(k, spot):
+        parts = []
+        for expert in (plane, near_plane):
+            weight = table[k, pl.ds(8 + expert, 1), :]
+            parts.append(jnp.where(matches(k, expert), weight, 0.0))
+        weight = jnp.transpose(jnp.concatenate(parts, axis=0))
+        high = weight.astype(jnp.bfloat16)
+        mix[spot, 0] = high
+        mix[spot, 1] = (weight - high.astype(jnp.float32)).astype(jnp.bfloat16)
+
+    def select(k, block):
+        return jnp.dot(picks[k], block, preferred_element_type=jnp.float32).astype(x.dtype)
+
+    def mixed(spot, own, other):
+        both = jnp.concatenate([own, other], axis=0)
+        total = jnp.dot(mix[spot, 0], both, preferred_element_type=jnp.float32)
+        return total + jnp.dot(mix[spot, 1], both, preferred_element_type=jnp.float32)
+
+    set_pick(0)
+    set_mix(0, 0)
+    pl.semaphore_wait(barrier, len(peers))
+
+    table_y = remote(table.at[0], table.at[1], table_send.at[0], table_recv.at[0], neighbour)
+    table_f = remote(table.at[0], table.at[2 + kind], table_send.at[1], table_recv.at[1 + kind], far)
+    table_y.start()
+    table_f.start()
+
+    def table_arrival(k):
+        return remote(table.at[0], table.at[k], table_send.at[0], table_recv.at[k - 1], far)
+
+    def cross_copy(q):
+        cols = columns(q)
+        return remote(tokens.at[:, cols], raw_y.at[:, cols], cross_send.at[q], cross_recv.at[q], neighbour)
+
+    def far_copy(q, k):
+        cols = columns(q)
+        return remote(tokens.at[:, cols], raw_f.at[k, :, cols], far_send.at[q], far_recv.at[k, q], far)
+
+    def near_copy(k, q):
+        cols, slot = columns(q), s if k == 0 else cross_s
+        return remote(
+            near_stage.at[:, cols], x.at[near_j, slot, :, cols],
+            near_send.at[k, q], near_recv.at[k, q], near,
+        )
+
+    def fwd_copy(i, q):
+        cols = columns(q)
+        return remote(
+            far_stage.at[:, cols], x.at[2 + i, s, :, cols], fwd_send.at[i, q], fwd_recv.at[i, q], near
+        )
+
+    def y_copy(i, q):
+        cols = columns(q)
+        return remote(
+            x.at[2 + i, s, :, cols], x.at[2 + i, s, :, cols], y_send.at[i, q], y_recv.at[i, q], neighbour
+        )
+
+    def y_arrival(i, q):
+        cols = columns(q)
+        return remote(
+            x.at[2 + i, s, :, cols], x.at[2 + i, cross_s, :, cols],
+            y_send.at[i, q], y_recv.at[i, q], neighbour,
+        )
+
+    def d_copy(j, r, q):
+        cols, slot = columns(q), r * 2 + core
+        return remote(
+            x.at[j, slot, :, cols], x.at[j, slot, :, cols], d_send.at[j, r], d_recv.at[j, r], partner
+        )
+
+    def d_whole(j, r, lane_core):
+        slot = r * 2 + lane_core
+        return remote(x.at[j, slot], x.at[j, slot], d_send.at[j, r], d_recv.at[j, r], partner)
+
+    def gathered(j):
+        for r in range(2):
+            d_whole(j, r, 1 - core).wait_recv()
+
+    def rp_copy(j, t, q, k, slot):
+        cols = columns(q)
+        return remote(
+            x.at[j, slot, :, cols], pair.at[t, k, :, cols],
+            rp_send.at[j, q, k], rp_recv.at[j, q, k], partner,
+        )
+
+    def ry_copy(j, t, q):
+        cols = columns(q)
+        return remote(
+            x.at[j, cross_s, :, cols], cross.at[t, :, cols],
+            ry_send.at[j, q], ry_recv.at[j, q], neighbour,
+        )
+
+    def nr_copy(q):
+        cols = columns(q)
+        return remote(x.at[near_j, s, :, cols], near_ret.at[:, cols], nr_send.at[q], nr_recv.at[q], near)
+
+    def or_copy(i, q):
+        cols = columns(q)
+        return remote(
+            x.at[2 + i, s, :, cols], outer_ret.at[i, :, cols], or_send.at[i, q], or_recv.at[i, q], near
+        )
+
+    def fr_copy(i, q):
+        cols = columns(q)
+        return remote(
+            raw_f.at[i, :, cols], far_ret.at[:, cols], fr_send.at[i, q], fr_recv.at[q],
+            far if i == 0 else far_b,
+        )
+
+    def out_copy(q):
+        cols = columns(q)
+        return pltpu.make_async_copy(raw.at[:, cols], out_hbm.at[:, cols], out_sem.at[q])
+
+    def expand(j, spot):
+        @each
+        def _(q):
+            cols = columns(q)
+            part = x[j, :, :, cols].reshape(rows, tile)
+
+            @pl.when(q == 0)
+            def _():
+                acc[...] = jnp.zeros_like(acc)
+
+            acc[0] += jnp.dot(part, gate[cols, :], preferred_element_type=jnp.float32)
+            acc[1] += jnp.dot(part, up[cols, :], preferred_element_type=jnp.float32)
+
+        value = acc[0]
+        hidden[spot] = (value / (1.0 + jnp.exp(-value)) * acc[1]).astype(hidden.dtype)
+
+    def contract(j, t, spot, credit):
+        for r in range(2):
+            d_whole(j, r, core).wait_send()
+        if j >= 2:
+            @each
+            def _(q):
+                y_copy(j - 2, q).wait_send()
+        if credit:
+            pl.semaphore_wait(pair_free, 1)
+            pl.semaphore_wait(cross_free, 1)
+
+        @pl.loop(0, chunks + 1)
+        def _(q):
+            @pl.when(q < chunks)
+            def _():
+                cols = columns(q)
+                part = jnp.dot(hidden[spot], down[:, cols], preferred_element_type=jnp.float32)
+                x[j, :, :, cols] = part.astype(x.dtype).reshape(SHARDS, cap, tile)
+                rp_copy(j, t, q, 1 - row, diag_s).start()
+                rp_copy(j, t, q, row, partner_s).start()
+
+            @pl.when(q > 0)
+            def _():
+                cols = columns(q - 1)
+                rp_copy(j, t, q - 1, 1 - row, diag_s).wait_recv()
+                total = x[j, cross_s, :, cols].astype(jnp.float32)
+                total += pair[t, 1 - row, :, cols].astype(jnp.float32)
+                x[j, cross_s, :, cols] = total.astype(x.dtype)
+                ry_copy(j, t, q - 1).start()
+
+    def finish(j, t, credit, then):
+        @each
+        def _(q):
+            cols = columns(q)
+            rp_copy(j, t, q, row, partner_s).wait_recv()
+            total = x[j, s, :, cols].astype(jnp.float32) + pair[t, row, :, cols].astype(jnp.float32)
+            ry_copy(j, t, q).wait_recv()
+            x[j, s, :, cols] = (total + cross[t, :, cols].astype(jnp.float32)).astype(x.dtype)
+            then(q)
+
+        if credit:
+            pl.semaphore_signal(pair_free, inc=1, device_id={"expert": partner}, device_id_type=MESH)
+            pl.semaphore_signal(cross_free, inc=1, device_id={"expert": neighbour}, device_id_type=MESH)
+
+    def to_inner(i):
+        def then(q):
+            @pl.when(outer)
+            def _():
+                or_copy(i, q).start()
+
+        return then
+
+    def merge(i):
+        @pl.when(inner)
+        def _():
+            @each
+            def _(q):
+                cols = columns(q)
+                or_copy(i, q).wait_recv()
+                total = mixed(1 + i, x[2 + i, s, :, cols], outer_ret[i, :, cols])
+                raw_f[i, :, cols] = total.astype(raw_f.dtype)
+                fr_copy(i, q).start()
+
+    def enter(i, q):
+        cols = columns(q)
+
+        @pl.when(inner)
+        def _():
+            far_copy(q, i).wait_recv()
+            taken = select(2 + i, raw_f[i, :, cols])
+            x[2 + i, s, :, cols] = taken[:cap]
+            if i > 0:
+                fwd_copy(i - 1, q).wait_send()
+            far_stage[:, cols] = taken[cap:]
+            fwd_copy(i, q).start()
+
+        @pl.when(outer)
+        def _():
+            fwd_copy(i, q).wait_recv()
+
+        y_copy(i, q).start()
+        d_copy(2 + i, row, q).start()
+
+    each(lambda q: cross_copy(q).start())
+
+    @pl.when(inner)
+    def _():
+        each(lambda q: far_copy(q, 0).start())
+
+    for load in loads:
+        load.start()
+    raw_load.wait()
+
+    @each
+    def _(q):
+        cols = columns(q)
+        taken = select(0, raw[:, cols])
+        near_stage[:, cols] = taken[cap:]
+        near_copy(0, q).start()
+        x[own_j, s, :, cols] = taken[:cap]
+        d_copy(own_j, row, q).start()
+
+    @pl.when(outer)
+    def _():
+        each(lambda q: far_copy(q, 1).start())
+
+    table_arrival(1).wait_recv()
+    set_pick(1)
+
+    @pl.when(inner)
+    def _():
+        for i in range(2):
+            table_arrival(2 + i).wait_recv()
+            set_pick(2 + i)
+            set_mix(2 + i, 1 + i)
+
+    @each
+    def _(q):
+        cols = columns(q)
+        cross_copy(q).wait_recv()
+        taken = select(1, raw_y[:, cols])
+        near_copy(0, q).wait_send()
+        near_stage[:, cols] = taken[cap:]
+        near_copy(1, q).start()
+        x[own_j, cross_s, :, cols] = taken[:cap]
+        d_copy(own_j, 1 - row, q).start()
+        enter(0, q)
+
+    loads[0].wait()
+    loads[1].wait()
+    gathered(own_j)
+    expand(own_j, 0)
+
+    @each
+    def _(q):
+        enter(1, q)
+        y_arrival(0, q).wait_recv()
+        d_copy(2, 1 - row, q).start()
+
+    gathered(2)
+    expand(2, 1)
+    loads[2].wait()
+    contract(2, 0, 1, False)
+
+    @each
+    def _(q):
+        y_arrival(1, q).wait_recv()
+        d_copy(3, 1 - row, q).start()
+
+    gathered(3)
+    expand(3, 1)
+    contract(3, 1, 1, False)
+    finish(2, 0, True, to_inner(0))
+    contract(own_j, 0, 0, True)
+    merge(0)
+
+    @each
+    def _(q):
+        for k in range(2):
+            near_copy(k, q).wait_recv()
+            d_copy(near_j, row if k == 0 else 1 - row, q).start()
+
+    gathered(near_j)
+    expand(near_j, 1)
+    finish(3, 1, True, to_inner(1))
+    contract(near_j, 1, 1, True)
+    merge(1)
+    finish(own_j, 0, False, lambda q: None)
+    finish(near_j, 1, False, lambda q: nr_copy(q).start())
+
+    @each
+    def _(q):
+        cols = columns(q)
+        nr_copy(q).wait_recv()
+        fr_copy(0, q).wait_recv()
+        total = mixed(0, x[own_j, s, :, cols], near_ret[:, cols])
+        raw[:, cols] = (total + far_ret[:, cols].astype(jnp.float32)).astype(raw.dtype)
+        out_copy(q).start()
+
+    table_y.wait_send()
+    table_f.wait_send()
+
+    @each
+    def _(q):
+        cross_copy(q).wait_send()
+        far_copy(q, 0).wait_send()
+        near_copy(1, q).wait_send()
+        nr_copy(q).wait_send()
+        for j, t in ((0, 0), (1, 1), (2, 0), (3, 1)):
+            rp_copy(j, t, q, 1 - row, diag_s).wait_send()
+            rp_copy(j, t, q, row, partner_s).wait_send()
+            ry_copy(j, t, q).wait_send()
+
+        @pl.when(inner)
+        def _():
+            fwd_copy(1, q).wait_send()
+            fr_copy(0, q).wait_send()
+            fr_copy(1, q).wait_send()
+
+        @pl.when(outer)
+        def _():
+            or_copy(0, q).wait_send()
+            or_copy(1, q).wait_send()
+
+        out_copy(q).wait()
+
+
+def routed(tokens, route_ids, levels, w_gate, w_up, w_down, cap):
+    tok_rows, width = tokens.shape
+    ff, dtype = w_gate.shape[2], tokens.dtype
+    rows, chunks = SHARDS * cap, width // tile_of(width, 1024)
+    dma, vmem = pltpu.SemaphoreType.DMA, pltpu.VMEM
+    anywhere, local = pl.BlockSpec(memory_space=pl.ANY), pl.BlockSpec(memory_space=pltpu.VMEM)
+    return pl.pallas_call(
+        routed_kernel,
+        out_shape=jax.ShapeDtypeStruct((tok_rows, width), dtype),
+        in_specs=[anywhere, local, local, anywhere, anywhere, anywhere],
+        out_specs=anywhere,
+        scratch_shapes=[
+            vmem((4, SHARDS, cap, width), dtype),
+            vmem((width, ff), dtype),
+            vmem((width, ff), dtype),
+            vmem((ff, width), dtype),
+            vmem((2, rows, ff), jnp.float32),
+            vmem((2, rows, ff), dtype),
+            vmem((2, 2, cap, width), dtype),
+            vmem((2, cap, width), dtype),
+            vmem((tok_rows, width), dtype),
+            vmem((tok_rows, width), dtype),
+            vmem((2, tok_rows, width), dtype),
+            vmem((cap, width), dtype),
+            vmem((cap, width), dtype),
+            vmem((cap, width), dtype),
+            vmem((2, cap, width), dtype),
+            vmem((tok_rows, width), dtype),
+            vmem((4, 16, tok_rows), jnp.float32),
+            vmem((4, 2 * cap, tok_rows), dtype),
+            vmem((3, 2, tok_rows, 2 * cap), dtype),
+            dma((3,)), dma, dma((chunks,)), dma((2,)), dma((3,)),
+            dma((chunks,)), dma((chunks,)), dma((chunks,)), dma((2, chunks)),
+            dma((2, chunks)), dma((2, chunks)),
+            dma((2, chunks)), dma((2, chunks)),
+            dma((2, chunks)), dma((2, chunks)),
+            dma((4, 2)), dma((4, 2)),
+            dma((4, chunks, 2)), dma((4, chunks, 2)),
+            dma((4, chunks)), dma((4, chunks)),
+            dma((chunks,)), dma((chunks,)),
+            dma((2, chunks)), dma((2, chunks)),
+            dma((2, chunks)), dma((chunks,)),
+            pltpu.SemaphoreType.REGULAR, pltpu.SemaphoreType.REGULAR,
+        ],
+        compiler_params=pltpu.CompilerParams(
+            collective_id=0, has_side_effects=True, vmem_limit_bytes=67_000_000
+        ),
+    )(tokens, route_ids, levels, w_gate, w_up, w_down)
+
+
 def combine_kernel(weight_ref, ret_ref, out_ref):
     weight = weight_ref[...]
     high = weight.astype(jnp.bfloat16)
@@ -236,6 +700,8 @@
     cap = -(-capacity // 16) * 16
     slots = experts * cap
     dtype = tokens.dtype
+    if experts == 4 and top == 2 and tok_rows < 2 * cap:
+        return routed(tokens, route_ids, levels, w_gate, w_up, w_down, cap)
 
     chosen = route_ids[:, :, None] == jnp.arange(experts, dtype=jnp.int32)
     named = jnp.any(chosen, axis=1)

time: 268 us -> 271 us (1.011)
  Pallas kernels: 259 us -> 265 us
  local copies, waits for them, and re-layouts: 0.39 us -> 5.66 us
  matrix products: 5.18 us -> 0 us
  other arithmetic: 3.5 us -> 0 us
    pallas_call x2 -> x1, Pallas kernels: 259 us -> 265 us  [routed(): pl.pallas_call(routed_kernel, out_shape=jax.ShapeDtypeStruct((tok_rows, w...]
    unnamed x0 -> x3, local copies, waits for them, and re-layouts: none -> 5.66 us
    dot_general x2 -> x0, matrix products: 5.18 us -> none  [the longest x1 5.04 us: on_device(): lax.dot_general(pick.astype(dtype), tokens, (((0,), (0,)), ((), ())), pre...]
where the time goes in v1:
time: 271 us
  Pallas kernels  265 us (98%)
  local copies, waits for them, and re-layouts  5.66 us (2%)
    pallas_call x1, Pallas kernels, routed(): pl.pallas_call(routed_kernel, out_shape=jax.ShapeDtypeStruct((tok_rows, w...  265 us
    unnamed x3, local copies, waits for them, and re-layouts  5.66 us

profile of v1, /device:TPU:0, one launch (start us, length us, event | category | flops | bytes accessed | tf_op | source)
XLA Modules:
  0.0 271.1 jit_solution(17624516540187771186)
XLA Ops:
  0.0 1.4 copy.7.ids
  1.4 1.4 copy.8.levels
  2.8 265.4 %shard_map.64 = bf16[128,7168]{1,0:T(8,128)(2,1)} custom-call(bf16[128,7168]{1,0:T(8,128)(2,1)} %tokens.1, s32[128,2]{1,0:T(8,128)} %copy.7.ids, s32[128,2]{1,0:T(8,128)} %copy.8.levels, bf16[1,7168,512]{2,1,0:T(8,128)(2,1)} %gate_hbm.1, bf16[1,7168,512]{2,1,0:T(8,128)(2,1)} %up_hbm.1, bf16[1,512,7168]{2,1,0:T(8,128)(2,1)} %down_hbm.1), custom_call_target="tpu_custom_call" | custom-call | tf_op jit(solution)/shard_map/pallas_call | solution.py:641
  268.3 2.8 %copy.10 = bf16[128,7168]{1,0:T(8,128)(2,1)} copy(bf16[128,7168]{1,0:T(8,128)(2,1)} %shard_map.64) | data formatting | bytes 3670016

commit v2 on v1

--- a/solution.py
+++ b/solution.py
@@ -221,7 +221,7 @@
 def routed_kernel(
     tokens, ids, levels, gate_hbm, up_hbm, down_hbm, out_hbm,
     x, gate, up, down, acc, hidden, pair, cross, raw, raw_y, raw_f,
-    near_stage, far_stage, near_ret, outer_ret, far_ret, table, picks, mix,
+    near_stage, near_ret, outer_ret, far_ret, table, picks, mix,
     w_sem, raw_sem, out_sem, table_send, table_recv,
     cross_send, cross_recv, far_send, far_recv, near_send, near_recv,
     fwd_send, fwd_recv, y_send, y_recv, d_send, d_recv,
@@ -276,16 +276,16 @@
 
     lane = lax.broadcasted_iota(jnp.int32, (tok_rows, tok_rows), 1)
     line = lax.broadcasted_iota(jnp.int32, (tok_rows, tok_rows), 0)
-    first, second = ids[:, 0:1] == lane, ids[:, 1:2] == lane
-    level_0, level_1 = levels[:, 0:1].astype(jnp.float32), levels[:, 1:2].astype(jnp.float32)
+    expert_of = lax.broadcasted_iota(jnp.int32, (8, tok_rows), 0)
+    first, second = ids[0:1, :] == expert_of, ids[1:2, :] == expert_of
+    level_0, level_1 = levels[0:1, :].astype(jnp.float32), levels[1:2, :].astype(jnp.float32)
     named = jnp.where(first | second, 1.0, 0.0)
-    earlier = jnp.where(line > lane, 1.0, 0.0).astype(jnp.bfloat16)
-    rank = jnp.dot(earlier, named.astype(jnp.bfloat16), preferred_element_type=jnp.float32)
-    place = jnp.where(named > 0.0, rank, 2.0 * tok_rows)
+    earlier = jnp.where(line < lane, 1.0, 0.0).astype(jnp.bfloat16)
+    rank = jnp.dot(named.astype(jnp.bfloat16), earlier, preferred_element_type=jnp.float32)
     share = jnp.where(first, level_0 / (level_0 + level_1), 0.0)
     share += jnp.where(second, level_1 / (level_0 + level_1), 0.0)
-    table[0, 0:8, :] = jnp.transpose(place)[0:8, :]
-    table[0, 8:16, :] = jnp.transpose(share)[0:8, :]
+    table[0, 0:8, :] = jnp.where(named > 0.0, rank, 2.0 * tok_rows)
+    table[0, 8:16, :] = share
 
     def matches(k, expert):
         spot = lax.broadcasted_iota(jnp.int32, (cap, tok_rows), 0).astype(jnp.float32)
@@ -319,7 +319,7 @@
     pl.semaphore_wait(barrier, len(peers))
 
     table_y = remote(table.at[0], table.at[1], table_send.at[0], table_recv.at[0], neighbour)
-    table_f = remote(table.at[0], table.at[2 + kind], table_send.at[1], table_recv.at[1 + kind], far)
+    table_f = remote(table.at[0], table.at[3 - kind], table_send.at[1], table_recv.at[2 - kind], far)
     table_y.start()
     table_f.start()
 
@@ -328,23 +328,23 @@
 
     def cross_copy(q):
         cols = columns(q)
-        return remote(tokens.at[:, cols], raw_y.at[:, cols], cross_send.at[q], cross_recv.at[q], neighbour)
+        return remote(raw.at[:, cols], raw_y.at[:, cols], cross_send.at[q], cross_recv.at[q], neighbour)
 
     def far_copy(q, k):
         cols = columns(q)
-        return remote(tokens.at[:, cols], raw_f.at[k, :, cols], far_send.at[q], far_recv.at[k, q], far)
+        return remote(raw.at[:, cols], raw_f.at[k, :, cols], far_send.at[q], far_recv.at[k, q], far)
 
     def near_copy(k, q):
         cols, slot = columns(q), s if k == 0 else cross_s
         return remote(
-            near_stage.at[:, cols], x.at[near_j, slot, :, cols],
+            near_stage.at[k, :, cols], x.at[near_j, slot, :, cols],
             near_send.at[k, q], near_recv.at[k, q], near,
         )
 
     def fwd_copy(i, q):
         cols = columns(q)
         return remote(
-            far_stage.at[:, cols], x.at[2 + i, s, :, cols], fwd_send.at[i, q], fwd_recv.at[i, q], near
+            raw_f.at[i, pl.ds(0, cap), cols], x.at[2 + i, s, :, cols], fwd_send.at[i, q], fwd_recv.at[i, q], near
         )
 
     def y_copy(i, q):
@@ -402,7 +402,7 @@
         cols = columns(q)
         return remote(
             raw_f.at[i, :, cols], far_ret.at[:, cols], fr_send.at[i, q], fr_recv.at[q],
-            far if i == 0 else far_b,
+            far_b if i == 0 else far,
         )
 
     def out_copy(q):
@@ -425,7 +425,7 @@
         value = acc[0]
         hidden[spot] = (value / (1.0 + jnp.exp(-value)) * acc[1]).astype(hidden.dtype)
 
-    def contract(j, t, spot, credit):
+    def contract(j, t, spot, credit, also):
         for r in range(2):
             d_whole(j, r, core).wait_send()
         if j >= 2:
@@ -445,6 +445,8 @@
                 x[j, :, :, cols] = part.astype(x.dtype).reshape(SHARDS, cap, tile)
                 rp_copy(j, t, q, 1 - row, diag_s).start()
                 rp_copy(j, t, q, row, partner_s).start()
+                for step in also:
+                    step(q)
 
             @pl.when(q > 0)
             def _():
@@ -455,162 +457,205 @@
                 x[j, cross_s, :, cols] = total.astype(x.dtype)
                 ry_copy(j, t, q - 1).start()
 
-    def finish(j, t, credit, then):
-        @each
-        def _(q):
+    def finish(j, t):
+        def step(q):
             cols = columns(q)
             rp_copy(j, t, q, row, partner_s).wait_recv()
             total = x[j, s, :, cols].astype(jnp.float32) + pair[t, row, :, cols].astype(jnp.float32)
             ry_copy(j, t, q).wait_recv()
             x[j, s, :, cols] = (total + cross[t, :, cols].astype(jnp.float32)).astype(x.dtype)
-            then(q)
-
-        if credit:
-            pl.semaphore_signal(pair_free, inc=1, device_id={"expert": partner}, device_id_type=MESH)
-            pl.semaphore_signal(cross_free, inc=1, device_id={"expert": neighbour}, device_id_type=MESH)
-
-    def to_inner(i):
-        def then(q):
-            @pl.when(outer)
-            def _():
-                or_copy(i, q).start()
-
-        return then
+            if j >= 2:
+                @pl.when(outer)
+                def _():
+                    or_copy(j - 2, q).start()
+            elif j == near_j:
+                nr_copy(q).start()
+
+        return step
+
+    def release():
+        pl.semaphore_signal(pair_free, inc=1, device_id={"expert": partner}, device_id_type=MESH)
+        pl.semaphore_signal(cross_free, inc=1, device_id={"expert": neighbour}, device_id_type=MESH)
 
     def merge(i):
-        @pl.when(inner)
-        def _():
-            @each
-            def _(q):
+        def step(q):
+            @pl.when(inner)
+            def _():
                 cols = columns(q)
                 or_copy(i, q).wait_recv()
                 total = mixed(1 + i, x[2 + i, s, :, cols], outer_ret[i, :, cols])
+                fwd_copy(i, q).wait_send()
                 raw_f[i, :, cols] = total.astype(raw_f.dtype)
                 fr_copy(i, q).start()
 
+        return step
+
+    def lagged(i):
+        def step(q):
+            pl.when(q >= 2)(lambda: merge(i)(q - 2))
+
+        return step
+
+    def merge_rest(i):
+        pl.loop(chunks - 2, chunks)(merge(i))
+
     def enter(i, q):
         cols = columns(q)
 
         @pl.when(inner)
         def _():
-            far_copy(q, i).wait_recv()
+            with jax.named_scope("w_far"):
+                far_copy(q, i).wait_recv()
             taken = select(2 + i, raw_f[i, :, cols])
             x[2 + i, s, :, cols] = taken[:cap]
-            if i > 0:
-                fwd_copy(i - 1, q).wait_send()
-            far_stage[:, cols] = taken[cap:]
+            raw_f[i, 0:cap, cols] = taken[cap:]
             fwd_copy(i, q).start()
 
         @pl.when(outer)
         def _():
-            fwd_copy(i, q).wait_recv()
+            with jax.named_scope("w_fwd"):
+                fwd_copy(i, q).wait_recv()
 
         y_copy(i, q).start()
         d_copy(2 + i, row, q).start()
 
-    each(lambda q: cross_copy(q).start())
-
-    @pl.when(inner)
-    def _():
-        each(lambda q: far_copy(q, 0).start())
-
-    for load in loads:
-        load.start()
-    raw_load.wait()
-
-    @each
-    def _(q):
-        cols = columns(q)
-        taken = select(0, raw[:, cols])
-        near_stage[:, cols] = taken[cap:]
-        near_copy(0, q).start()
-        x[own_j, s, :, cols] = taken[:cap]
-        d_copy(own_j, row, q).start()
-
-    @pl.when(outer)
-    def _():
-        each(lambda q: far_copy(q, 1).start())
-
-    table_arrival(1).wait_recv()
-    set_pick(1)
-
-    @pl.when(inner)
-    def _():
-        for i in range(2):
+    def far_table(i):
+        @pl.when(inner)
+        def _():
             table_arrival(2 + i).wait_recv()
             set_pick(2 + i)
             set_mix(2 + i, 1 + i)
 
+    raw_load.wait()
+    each(lambda q: cross_copy(q).start())
+    each(lambda q: far_copy(q, 1 - kind).start())
+    for load in loads:
+        load.start()
+
+    with jax.named_scope("take_own"):
+        @each
+        def _(q):
+            cols = columns(q)
+            taken = select(0, raw[:, cols])
+            near_stage[0, :, cols] = taken[cap:]
+            x[own_j, s, :, cols] = taken[:cap]
+            d_copy(own_j, row, q).start()
+
+            @pl.when(outer | (q < 2))
+            def _():
+                near_copy(0, q).start()
+
+    with jax.named_scope("tables"):
+        table_arrival(1).wait_recv()
+        set_pick(1)
+
+        far_table(0)
+
+    with jax.named_scope("enter_b"):
+        @each
+        def _(q):
+            cols = columns(q)
+            with jax.named_scope("w_cross"):
+                cross_copy(q).wait_recv()
+            taken = select(1, raw_y[:, cols])
+            near_stage[1, :, cols] = taken[cap:]
+            x[own_j, cross_s, :, cols] = taken[:cap]
+            d_copy(own_j, 1 - row, q).start()
+            enter(0, q)
+
+            pl.when(outer)(lambda: near_copy(1, q).start())
+            pl.when(inner & (q % 2 == 1))(lambda: near_copy(0, 2 + q // 2).start())
+
+    with jax.named_scope("wait_own"):
+        loads[0].wait()
+        loads[1].wait()
+        gathered(own_j)
+    with jax.named_scope("expand_own"):
+        expand(own_j, 0)
+
+    with jax.named_scope("enter_a"):
+        far_table(1)
+
+        @each
+        def _(q):
+            enter(1, q)
+            with jax.named_scope("w_yb"):
+                y_arrival(0, q).wait_recv()
+            d_copy(2, 1 - row, q).start()
+
+            late = 2 + chunks // 2 + q // 2
+
+            @pl.when(inner & (q % 2 == 1) & (late < chunks))
+            def _():
+                near_copy(0, late).start()
+
+    pl.when(inner)(lambda: each(lambda q: near_copy(1, q).start()))
+
+    with jax.named_scope("wait_b"):
+        gathered(2)
+    with jax.named_scope("expand_b"):
+        expand(2, 1)
+    loads[2].wait()
+    with jax.named_scope("contract_b"):
+        contract(2, 0, 1, False, ())
+
+    with jax.named_scope("wait_a"):
+        @each
+        def _(q):
+            y_arrival(1, q).wait_recv()
+            d_copy(3, 1 - row, q).start()
+
+        gathered(3)
+    with jax.named_scope("expand_a"):
+        expand(3, 1)
+    with jax.named_scope("contract_a"):
+        contract(3, 1, 1, False, (finish(2, 0), lagged(0)))
+        release()
+    with jax.named_scope("merge_b"):
+        merge_rest(0)
+
+    with jax.named_scope("contract_own"):
+        contract(own_j, 0, 0, True, (finish(3, 1), lagged(1)))
+        release()
+    with jax.named_scope("merge_a"):
+        merge_rest(1)
+
+    with jax.named_scope("wait_near"):
+        @each
+        def _(q):
+            for k in range(2):
+                near_copy(k, q).wait_recv()
+                d_copy(near_j, row if k == 0 else 1 - row, q).start()
+
+        gathered(near_j)
+    with jax.named_scope("expand_near"):
+        expand(near_j, 1)
+    with jax.named_scope("contract_near"):
+        contract(near_j, 1, 1, True, (finish(own_j, 0),))
+
+    with jax.named_scope("finish_near"):
+        each(finish(near_j, 1))
+
+    with jax.named_scope("combine"):
+        @each
+        def _(q):
+            cols = columns(q)
+            cross_copy(q).wait_send()
+            far_copy(q, 0).wait_send()
+            with jax.named_scope("w_nr"):
+                nr_copy(q).wait_recv()
+            with jax.named_scope("w_fr"):
+                fr_copy(0, q).wait_recv()
+            total = mixed(0, x[own_j, s, :, cols], near_ret[:, cols])
+            raw[:, cols] = (total + far_ret[:, cols].astype(jnp.float32)).astype(raw.dtype)
+            out_copy(q).start()
+
+    table_y.wait_send()
+    table_f.wait_send()
+
     @each
     def _(q):
-        cols = columns(q)
-        cross_copy(q).wait_recv()
-        taken = select(1, raw_y[:, cols])
         near_copy(0, q).wait_send()
-        near_stage[:, cols] = taken[cap:]
-        near_copy(1, q).start()
-        x[own_j, cross_s, :, cols] = taken[:cap]
-        d_copy(own_j, 1 - row, q).start()
-        enter(0, q)
-
-    loads[0].wait()
-    loads[1].wait()
-    gathered(own_j)
-    expand(own_j, 0)
-
-    @each
-    def _(q):
-        enter(1, q)
-        y_arrival(0, q).wait_recv()
-        d_copy(2, 1 - row, q).start()
-
-    gathered(2)
-    expand(2, 1)
-    loads[2].wait()
-    contract(2, 0, 1, False)
-
-    @each
-    def _(q):
-        y_arrival(1, q).wait_recv()
-        d_copy(3, 1 - row, q).start()
-
-    gathered(3)
-    expand(3, 1)
-    contract(3, 1, 1, False)
-    finish(2, 0, True, to_inner(0))
-    contract(own_j, 0, 0, True)
-    merge(0)
-
-    @each
-    def _(q):
-        for k in range(2):
-            near_copy(k, q).wait_recv()
-            d_copy(near_j, row if k == 0 else 1 - row, q).start()
-
-    gathered(near_j)
-    expand(near_j, 1)
-    finish(3, 1, True, to_inner(1))
-    contract(near_j, 1, 1, True)
-    merge(1)
-    finish(own_j, 0, False, lambda q: None)
-    finish(near_j, 1, False, lambda q: nr_copy(q).start())
-
-    @each
-    def _(q):
-        cols = columns(q)
-        nr_copy(q).wait_recv()
-        fr_copy(0, q).wait_recv()
-        total = mixed(0, x[own_j, s, :, cols], near_ret[:, cols])
-        raw[:, cols] = (total + far_ret[:, cols].astype(jnp.float32)).astype(raw.dtype)
-        out_copy(q).start()
-
-    table_y.wait_send()
-    table_f.wait_send()
-
-    @each
-    def _(q):
-        cross_copy(q).wait_send()
-        far_copy(q, 0).wait_send()
         near_copy(1, q).wait_send()
         nr_copy(q).wait_send()
         for j, t in ((0, 0), (1, 1), (2, 0), (3, 1)):
@@ -620,7 +665,6 @@
 
         @pl.when(inner)
         def _():
-            fwd_copy(1, q).wait_send()
             fr_copy(0, q).wait_send()
             fr_copy(1, q).wait_send()
 
@@ -655,8 +699,7 @@
             vmem((tok_rows, width), dtype),
             vmem((tok_rows, width), dtype),
             vmem((2, tok_rows, width), dtype),
-            vmem((cap, width), dtype),
-            vmem((cap, width), dtype),
+            vmem((2, cap, width), dtype),
             vmem((cap, width), dtype),
             vmem((2, cap, width), dtype),
             vmem((tok_rows, width), dtype),
@@ -679,7 +722,7 @@
         compiler_params=pltpu.CompilerParams(
             collective_id=0, has_side_effects=True, vmem_limit_bytes=67_000_000
         ),
-    )(tokens, route_ids, levels, w_gate, w_up, w_down)
+    )(tokens, route_ids.T, levels.T, w_gate, w_up, w_down)
 
 
 def combine_kernel(weight_ref, ret_ref, out_ref):

time: 271 us -> 218 us (0.80)
  Pallas kernels: 265 us -> 215 us
  local copies, waits for them, and re-layouts: 5.66 us -> 2.85 us
    pallas_call x1, Pallas kernels: 265 us -> 215 us  [routed(): pl.pallas_call(routed_kernel, out_shape=jax.ShapeDtypeStruct((tok_rows, w...]
    unnamed x3 -> x1, local copies, waits for them, and re-layouts: 5.66 us -> 2.85 us
where the time goes in v2:
time: 218 us
  Pallas kernels  215 us (99%)
  local copies, waits for them, and re-layouts  2.85 us (1%)
    pallas_call x1, Pallas kernels, routed(): pl.pallas_call(routed_kernel, out_shape=jax.ShapeDtypeStruct((tok_rows, w...  215 us

profile of v2, /device:TPU:0, one launch (start us, length us, event | category | flops | bytes accessed | tf_op | source)
XLA Modules:
  0.0 218.2 jit_solution(13689259482728337456)
XLA Ops:
  0.0 215.3 %shard_map.64 = bf16[128,7168]{1,0:T(8,128)(2,1)} custom-call(bf16[128,7168]{1,0:T(8,128)(2,1)} %tokens.1, s32[2,128]{1,0:T(2,128)} %bitcast.2, s32[2,128]{1,0:T(2,128)} %bitcast.3, bf16[1,7168,512]{2,1,0:T(8,128)(2,1)} %gate_hbm.1, bf16[1,7168,512]{2,1,0:T(8,128)(2,1)} %up_hbm.1, bf16[1,512,7168]{2,1,0:T(8,128)(2,1)} %down_hbm.1), custom_call_target="tpu_custom_call" | custom-call | tf_op jit(solution)/shard_map/pallas_call | solution.py:685
  215.3 2.8 %copy.8 = bf16[128,7168]{1,0:T(8,128)(2,1)} copy(bf16[128,7168]{1,0:T(8,128)(2,1)} %shard_map.64) | data formatting | bytes 3670016

commit v3 on v2

--- a/solution.py
+++ b/solution.py
@@ -270,9 +270,13 @@
     raw_load.start()
 
     barrier = pltpu.get_barrier_semaphore()
-    peers = [partner, neighbour, near, far, far_b]
+    peers = [partner, neighbour, near, far]
     for peer in peers:
         pl.semaphore_signal(barrier, inc=1, device_id={"expert": peer}, device_id_type=MESH)
+
+    @pl.when(inner)
+    def _():
+        pl.semaphore_signal(barrier, inc=1, device_id={"expert": far_b}, device_id_type=MESH)
 
     lane = lax.broadcasted_iota(jnp.int32, (tok_rows, tok_rows), 1)
     line = lax.broadcasted_iota(jnp.int32, (tok_rows, tok_rows), 0)
@@ -316,7 +320,8 @@
 
     set_pick(0)
     set_mix(0, 0)
-    pl.semaphore_wait(barrier, len(peers))
+    with jax.named_scope("barrier"):
+        pl.semaphore_wait(barrier, len(peers) + 1 - kind)
 
     table_y = remote(table.at[0], table.at[1], table_send.at[0], table_recv.at[0], neighbour)
     table_f = remote(table.at[0], table.at[3 - kind], table_send.at[1], table_recv.at[2 - kind], far)
@@ -328,36 +333,36 @@
 
     def cross_copy(q):
         cols = columns(q)
-        return remote(raw.at[:, cols], raw_y.at[:, cols], cross_send.at[q], cross_recv.at[q], neighbour)
+        return remote(raw.at[:, cols], raw_y.at[:, cols], cross_send, cross_recv.at[q], neighbour)
 
     def far_copy(q, k):
         cols = columns(q)
-        return remote(raw.at[:, cols], raw_f.at[k, :, cols], far_send.at[q], far_recv.at[k, q], far)
+        return remote(raw.at[:, cols], raw_f.at[k, :, cols], far_send, far_recv.at[k, q], far)
 
     def near_copy(k, q):
         cols, slot = columns(q), s if k == 0 else cross_s
         return remote(
             near_stage.at[k, :, cols], x.at[near_j, slot, :, cols],
-            near_send.at[k, q], near_recv.at[k, q], near,
+            near_send.at[k], near_recv.at[k], near,
         )
 
     def fwd_copy(i, q):
         cols = columns(q)
         return remote(
-            raw_f.at[i, pl.ds(0, cap), cols], x.at[2 + i, s, :, cols], fwd_send.at[i, q], fwd_recv.at[i, q], near
+            raw_f.at[i, pl.ds(0, cap), cols], x.at[2 + i, s, :, cols], fwd_send.at[i], fwd_recv.at[i, q], near
         )
 
     def y_copy(i, q):
         cols = columns(q)
         return remote(
-            x.at[2 + i, s, :, cols], x.at[2 + i, s, :, cols], y_send.at[i, q], y_recv.at[i, q], neighbour
+            x.at[2 + i, s, :, cols], x.at[2 + i, s, :, cols], y_send.at[i], y_recv.at[i, q], neighbour
         )
 
     def y_arrival(i, q):
         cols = columns(q)
         return remote(
             x.at[2 + i, s, :, cols], x.at[2 + i, cross_s, :, cols],
-            y_send.at[i, q], y_recv.at[i, q], neighbour,
+            y_send.at[i], y_recv.at[i, q], neighbour,
         )
 
     def d_copy(j, r, q):
@@ -378,36 +383,36 @@
         cols = columns(q)
         return remote(
             x.at[j, slot, :, cols], pair.at[t, k, :, cols],
-            rp_send.at[j, q, k], rp_recv.at[j, q, k], partner,
+            rp_send.at[j], rp_recv.at[t, q, k], partner,
         )
 
     def ry_copy(j, t, q):
         cols = columns(q)
         return remote(
             x.at[j, cross_s, :, cols], cross.at[t, :, cols],
-            ry_send.at[j, q], ry_recv.at[j, q], neighbour,
+            ry_send.at[j], ry_recv.at[t, q], neighbour,
         )
 
     def nr_copy(q):
         cols = columns(q)
-        return remote(x.at[near_j, s, :, cols], near_ret.at[:, cols], nr_send.at[q], nr_recv.at[q], near)
+        return remote(x.at[near_j, s, :, cols], near_ret.at[:, cols], nr_send, nr_recv.at[q], near)
 
     def or_copy(i, q):
         cols = columns(q)
         return remote(
-            x.at[2 + i, s, :, cols], outer_ret.at[i, :, cols], or_send.at[i, q], or_recv.at[i, q], near
+            x.at[2 + i, s, :, cols], outer_ret.at[i, :, cols], or_send.at[i], or_recv.at[i, q], near
         )
 
     def fr_copy(i, q):
         cols = columns(q)
         return remote(
-            raw_f.at[i, :, cols], far_ret.at[:, cols], fr_send.at[i, q], fr_recv.at[q],
+            raw_f.at[i, :, cols], far_ret.at[:, cols], fr_send.at[i], fr_recv.at[q],
             far_b if i == 0 else far,
         )
 
     def out_copy(q):
         cols = columns(q)
-        return pltpu.make_async_copy(raw.at[:, cols], out_hbm.at[:, cols], out_sem.at[q])
+        return pltpu.make_async_copy(raw.at[:, cols], out_hbm.at[:, cols], out_sem)
 
     def expand(j, spot):
         @each
@@ -429,9 +434,7 @@
         for r in range(2):
             d_whole(j, r, core).wait_send()
         if j >= 2:
-            @each
-            def _(q):
-                y_copy(j - 2, q).wait_send()
+            remote(x.at[j, s], x.at[j, s], y_send.at[j - 2], d_recv.at[j, 0], neighbour).wait_send()
         if credit:
             pl.semaphore_wait(pair_free, 1)
             pl.semaphore_wait(cross_free, 1)
@@ -477,14 +480,23 @@
         pl.semaphore_signal(pair_free, inc=1, device_id={"expert": partner}, device_id_type=MESH)
         pl.semaphore_signal(cross_free, inc=1, device_id={"expert": neighbour}, device_id_type=MESH)
 
+    def sent(src, dst, send):
+        remote(src, dst, send, nr_recv.at[0], near).wait_send()
+
     def merge(i):
         def step(q):
             @pl.when(inner)
             def _():
                 cols = columns(q)
+
+                @pl.when(q == 0)
+                def _():
+                    sent(raw_f.at[i, pl.ds(0, cap)], near_ret, fwd_send.at[i])
+                    if i == 0:
+                        sent(near_stage.at[1], near_ret, near_send.at[1])
+
                 or_copy(i, q).wait_recv()
                 total = mixed(1 + i, x[2 + i, s, :, cols], outer_ret[i, :, cols])
-                fwd_copy(i, q).wait_send()
                 raw_f[i, :, cols] = total.astype(raw_f.dtype)
                 fr_copy(i, q).start()
 
@@ -526,7 +538,8 @@
             set_pick(2 + i)
             set_mix(2 + i, 1 + i)
 
-    raw_load.wait()
+    with jax.named_scope("w_raw"):
+        raw_load.wait()
     each(lambda q: cross_copy(q).start())
     each(lambda q: far_copy(q, 1 - kind).start())
     for load in loads:
@@ -573,28 +586,42 @@
     with jax.named_scope("expand_own"):
         expand(own_j, 0)
 
+    def enter_a(q):
+        enter(1, q)
+        y_arrival(0, q).wait_recv()
+        d_copy(2, 1 - row, q).start()
+        late = 2 + chunks // 2 + q // 2
+
+        @pl.when(inner & (q % 2 == 1) & (late < chunks))
+        def _():
+            near_copy(0, late).start()
+
+    middle = chunks // 2 + 1
     with jax.named_scope("enter_a"):
         far_table(1)
-
-        @each
-        def _(q):
-            enter(1, q)
-            with jax.named_scope("w_yb"):
-                y_arrival(0, q).wait_recv()
+        pl.loop(0, middle)(enter_a)
+
+        @pl.loop(middle, chunks)
+        def _(q):
+            y_arrival(0, q).wait_recv()
             d_copy(2, 1 - row, q).start()
-
-            late = 2 + chunks // 2 + q // 2
-
-            @pl.when(inner & (q % 2 == 1) & (late < chunks))
-            def _():
-                near_copy(0, late).start()
-
-    pl.when(inner)(lambda: each(lambda q: near_copy(1, q).start()))
 
     with jax.named_scope("wait_b"):
         gathered(2)
     with jax.named_scope("expand_b"):
         expand(2, 1)
+    with jax.named_scope("enter_a2"):
+        @pl.loop(middle, chunks)
+        def _(q):
+            enter(1, q)
+            late = 2 + chunks // 2 + q // 2
+
+            @pl.when(inner & (q % 2 == 1) & (late < chunks))
+            def _():
+                near_copy(0, late).start()
+
+        pl.when(inner)(lambda: each(lambda q: near_copy(1, q).start()))
+
     loads[2].wait()
     with jax.named_scope("contract_b"):
         contract(2, 0, 1, False, ())
@@ -614,34 +641,32 @@
     with jax.named_scope("merge_b"):
         merge_rest(0)
 
-    with jax.named_scope("contract_own"):
-        contract(own_j, 0, 0, True, (finish(3, 1), lagged(1)))
-        release()
-    with jax.named_scope("merge_a"):
-        merge_rest(1)
-
     with jax.named_scope("wait_near"):
-        @each
-        def _(q):
-            for k in range(2):
-                near_copy(k, q).wait_recv()
-                d_copy(near_j, row if k == 0 else 1 - row, q).start()
+        for k, r in ((0, row), (1, 1 - row)):
+            slot = r * 2 + core
+            remote(near_stage.at[k], x.at[near_j, slot], near_send.at[k], near_recv.at[k], near).wait_recv()
+            d_whole(near_j, r, core).start()
 
         gathered(near_j)
     with jax.named_scope("expand_near"):
         expand(near_j, 1)
     with jax.named_scope("contract_near"):
-        contract(near_j, 1, 1, True, (finish(own_j, 0),))
-
-    with jax.named_scope("finish_near"):
-        each(finish(near_j, 1))
+        contract(near_j, 0, 1, True, (finish(3, 1), lagged(1)))
+        release()
+    with jax.named_scope("merge_a"):
+        merge_rest(1)
+    with jax.named_scope("contract_own"):
+        contract(own_j, 1, 0, True, (finish(near_j, 0),))
 
     with jax.named_scope("combine"):
+        remote(raw, raw_y, cross_send, cross_recv.at[0], neighbour).wait_send()
+        remote(raw, raw_y, far_send, cross_recv.at[0], neighbour).wait_send()
+
         @each
         def _(q):
             cols = columns(q)
-            cross_copy(q).wait_send()
-            far_copy(q, 0).wait_send()
+            with jax.named_scope("w_own"):
+                finish(own_j, 1)(q)
             with jax.named_scope("w_nr"):
                 nr_copy(q).wait_recv()
             with jax.named_scope("w_fr"):
@@ -650,30 +675,28 @@
             raw[:, cols] = (total + far_ret[:, cols].astype(jnp.float32)).astype(raw.dtype)
             out_copy(q).start()
 
-    table_y.wait_send()
-    table_f.wait_send()
-
-    @each
-    def _(q):
-        near_copy(0, q).wait_send()
-        near_copy(1, q).wait_send()
-        nr_copy(q).wait_send()
-        for j, t in ((0, 0), (1, 1), (2, 0), (3, 1)):
-            rp_copy(j, t, q, 1 - row, diag_s).wait_send()
-            rp_copy(j, t, q, row, partner_s).wait_send()
-            ry_copy(j, t, q).wait_send()
+    with jax.named_scope("tail_sends"):
+        table_y.wait_send()
+        table_f.wait_send()
+        sent(near_stage.at[0], near_ret, near_send.at[0])
+        sent(x.at[near_j, s], near_ret, nr_send)
+        for j in range(4):
+            sent(x.at[j, pl.ds(0, 2)], pair.at[0], rp_send.at[j])
+            sent(x.at[j, cross_s], near_ret, ry_send.at[j])
 
         @pl.when(inner)
         def _():
-            fr_copy(0, q).wait_send()
-            fr_copy(1, q).wait_send()
+            for i in range(2):
+                sent(raw_f.at[i], far_ret, fr_send.at[i])
 
         @pl.when(outer)
         def _():
-            or_copy(0, q).wait_send()
-            or_copy(1, q).wait_send()
-
-        out_copy(q).wait()
+            sent(near_stage.at[1], near_ret, near_send.at[1])
+            for i in range(2):
+                sent(x.at[2 + i, s], near_ret, or_send.at[i])
+
+    with jax.named_scope("tail_out"):
+        pltpu.make_async_copy(raw, out_hbm, out_sem).wait()
 
 
 def routed(tokens, route_ids, levels, w_gate, w_up, w_down, cap):
@@ -706,17 +729,17 @@
             vmem((4, 16, tok_rows), jnp.float32),
             vmem((4, 2 * cap, tok_rows), dtype),
             vmem((3, 2, tok_rows, 2 * cap), dtype),
-            dma((3,)), dma, dma((chunks,)), dma((2,)), dma((3,)),
-            dma((chunks,)), dma((chunks,)), dma((chunks,)), dma((2, chunks)),
-            dma((2, chunks)), dma((2, chunks)),
-            dma((2, chunks)), dma((2, chunks)),
-            dma((2, chunks)), dma((2, chunks)),
+            dma((3,)), dma, dma, dma((2,)), dma((3,)),
+            dma, dma((chunks,)), dma, dma((2, chunks)),
+            dma((2,)), dma((2,)),
+            dma((2,)), dma((2, chunks)),
+            dma((2,)), dma((2, chunks)),
             dma((4, 2)), dma((4, 2)),
-            dma((4, chunks, 2)), dma((4, chunks, 2)),
-            dma((4, chunks)), dma((4, chunks)),
-            dma((chunks,)), dma((chunks,)),
-            dma((2, chunks)), dma((2, chunks)),
-            dma((2, chunks)), dma((chunks,)),
+            dma((4,)), dma((2, chunks, 2)),
+            dma((4,)), dma((2, chunks)),
+            dma, dma((chunks,)),
+            dma((2,)), dma((2, chunks)),
+            dma((2,)), dma((chunks,)),
             pltpu.SemaphoreType.REGULAR, pltpu.SemaphoreType.REGULAR,
         ],
         compiler_params=pltpu.CompilerParams(

time: 218 us -> 202 us (0.927)
  Pallas kernels: 215 us -> 198 us
    pallas_call x1, Pallas kernels: 215 us -> 198 us  [routed(): pl.pallas_call(routed_kernel, out_shape=jax.ShapeDtypeStruct((tok_rows, w...]
where the time goes in v3:
time: 202 us; the launch traced here: 201 us
  Pallas kernels  198 us (98%)
  local copies, waits for them, and re-layouts  2.85 us (1%)
    pallas_call x1, Pallas kernels, routed(): pl.pallas_call(routed_kernel, out_shape=jax.ShapeDtypeStruct((tok_rows, w...  198 us

profile of v3, /device:TPU:0, one launch (start us, length us, event | category | flops | bytes accessed | tf_op | source)
XLA Modules:
  0.0 200.8 jit_solution(15148324706269741244)
XLA Ops:
  0.0 197.9 %shard_map.64 = bf16[128,7168]{1,0:T(8,128)(2,1)} custom-call(bf16[128,7168]{1,0:T(8,128)(2,1)} %tokens.1, s32[2,128]{1,0:T(2,128)} %bitcast.2, s32[2,128]{1,0:T(2,128)} %bitcast.3, bf16[1,7168,512]{2,1,0:T(8,128)(2,1)} %gate_hbm.1, bf16[1,7168,512]{2,1,0:T(8,128)(2,1)} %up_hbm.1, bf16[1,512,7168]{2,1,0:T(8,128)(2,1)} %down_hbm.1), custom_call_target="tpu_custom_call" | custom-call | tf_op jit(solution)/shard_map/pallas_call | solution.py:708
  197.9 2.8 %copy.8 = bf16[128,7168]{1,0:T(8,128)(2,1)} copy(bf16[128,7168]{1,0:T(8,128)(2,1)} %shard_map.64) | data formatting | bytes 3670016

commit v4 on v3

--- a/solution.py
+++ b/solution.py
@@ -221,12 +221,13 @@
 def routed_kernel(
     tokens, ids, levels, gate_hbm, up_hbm, down_hbm, out_hbm,
     x, gate, up, down, acc, hidden, pair, cross, raw, raw_y, raw_f,
-    near_stage, near_ret, outer_ret, far_ret, table, picks, mix,
+    near_stage, near_ret, near_cross, outer_ret, far_ret, table, picks, mix,
     w_sem, raw_sem, out_sem, table_send, table_recv,
     cross_send, cross_recv, far_send, far_recv, near_send, near_recv,
     fwd_send, fwd_recv, y_send, y_recv, d_send, d_recv,
     rp_send, rp_recv, ry_send, ry_recv,
     nr_send, nr_recv, or_send, or_recv, fr_send, fr_recv,
+    nx_send, nx_recv, fin_send, fin_recv,
     pair_free, cross_free,
 ):
     me = lax.axis_index("expert")
@@ -248,6 +249,7 @@
     tile = tile_of(width, 1024)
     chunks = width // tile
     own_j, near_j = 0, 1
+    folds = near_cross.shape[0]
 
     def columns(q):
         return pl.ds(pl.multiple_of(q * tile, tile), tile)
@@ -414,7 +416,29 @@
         cols = columns(q)
         return pltpu.make_async_copy(raw.at[:, cols], out_hbm.at[:, cols], out_sem)
 
-    def expand(j, spot):
+    def folded(q):
+        return (q >= 2) & (q < 2 + folds)
+
+    def nx_copy(q):
+        return remote(
+            x.at[near_j, cross_s, :, columns(q)], near_cross.at[q - 2], nx_send, nx_recv.at[q - 2], near
+        )
+
+    def fin_copy(q):
+        return remote(
+            raw_y.at[:, columns(q)], raw_y.at[:, columns((q + folds) % chunks)],
+            fin_send, fin_recv.at[q - 2], neighbour,
+        )
+
+    def fold(q):
+        cols = columns(q)
+        with jax.named_scope("w_nx"):
+            nx_copy(q).wait_recv()
+        total = mixed(3, x[own_j, cross_s, :, cols], near_cross[q - 2])
+        raw_y[:, cols] = total.astype(raw_y.dtype)
+        fin_copy(q).start()
+
+    def expand(j, spot, also=()):
         @each
         def _(q):
             cols = columns(q)
@@ -426,6 +450,8 @@
 
             acc[0] += jnp.dot(part, gate[cols, :], preferred_element_type=jnp.float32)
             acc[1] += jnp.dot(part, up[cols, :], preferred_element_type=jnp.float32)
+            for step in also:
+                step(q)
 
         value = acc[0]
         hidden[spot] = (value / (1.0 + jnp.exp(-value)) * acc[1]).astype(hidden.dtype)
@@ -458,15 +484,35 @@
                 total = x[j, cross_s, :, cols].astype(jnp.float32)
                 total += pair[t, 1 - row, :, cols].astype(jnp.float32)
                 x[j, cross_s, :, cols] = total.astype(x.dtype)
-                ry_copy(j, t, q - 1).start()
+                if j >= 2:
+                    ry_copy(j, t, q - 1).start()
+                else:
+                    pl.when(~folded(q - 1))(lambda: ry_copy(j, t, q - 1).start())
+
+                    @pl.when(folded(q - 1))
+                    def _():
+                        nx_copy(q - 1).start() if j == near_j else fold(q - 1)
 
     def finish(j, t):
         def step(q):
             cols = columns(q)
-            rp_copy(j, t, q, row, partner_s).wait_recv()
+            with jax.named_scope("w_rp"):
+                rp_copy(j, t, q, row, partner_s).wait_recv()
             total = x[j, s, :, cols].astype(jnp.float32) + pair[t, row, :, cols].astype(jnp.float32)
-            ry_copy(j, t, q).wait_recv()
-            x[j, s, :, cols] = (total + cross[t, :, cols].astype(jnp.float32)).astype(x.dtype)
+
+            def whole():
+                with jax.named_scope("w_ry"):
+                    ry_copy(j, t, q).wait_recv()
+                x[j, s, :, cols] = (total + cross[t, :, cols].astype(jnp.float32)).astype(x.dtype)
+
+            def column_sum():
+                x[j, s, :, cols] = total.astype(x.dtype)
+
+            if j >= 2:
+                whole()
+            else:
+                pl.when(~folded(q))(whole)
+                pl.when(folded(q))(column_sum)
             if j >= 2:
                 @pl.when(outer)
                 def _():
@@ -495,21 +541,42 @@
                     if i == 0:
                         sent(near_stage.at[1], near_ret, near_send.at[1])
 
-                or_copy(i, q).wait_recv()
+                with jax.named_scope("w_or"):
+                    or_copy(i, q).wait_recv()
                 total = mixed(1 + i, x[2 + i, s, :, cols], outer_ret[i, :, cols])
                 raw_f[i, :, cols] = total.astype(raw_f.dtype)
                 fr_copy(i, q).start()
 
         return step
 
-    def lagged(i):
+    def early(j, t):
         def step(q):
-            pl.when(q >= 2)(lambda: merge(i)(q - 2))
+            pl.when(q == chunks // 2)(lambda: finish(j, t)(0))
+            pl.when(q == chunks - 1)(lambda: finish(j, t)(1))
 
         return step
 
-    def merge_rest(i):
-        pl.loop(chunks - 2, chunks)(merge(i))
+    def ahead(j, t):
+        def step(q):
+            pl.when(q < chunks - 2)(lambda: finish(j, t)(q + 2))
+
+        return step
+
+    def merge_most(i):
+        def step(q):
+            pl.when(q < chunks - 2)(lambda: merge(i)(q))
+
+        return step
+
+    def merge_last(i):
+        def step(q):
+            pl.when(q < 2)(lambda: merge(i)(chunks - 2 + q))
+
+        return step
+
+    def near_nth(n):
+        pl.when(n < chunks)(lambda: near_copy(0, n).start())
+        pl.when(n >= chunks)(lambda: near_copy(1, n - chunks).start())
 
     def enter(i, q):
         cols = columns(q)
@@ -561,6 +628,7 @@
     with jax.named_scope("tables"):
         table_arrival(1).wait_recv()
         set_pick(1)
+        set_mix(1, 3)
 
         far_table(0)
 
@@ -579,6 +647,8 @@
             pl.when(outer)(lambda: near_copy(1, q).start())
             pl.when(inner & (q % 2 == 1))(lambda: near_copy(0, 2 + q // 2).start())
 
+    pl.when(inner)(lambda: near_nth(2 + chunks // 2))
+
     with jax.named_scope("wait_own"):
         loads[0].wait()
         loads[1].wait()
@@ -590,11 +660,7 @@
         enter(1, q)
         y_arrival(0, q).wait_recv()
         d_copy(2, 1 - row, q).start()
-        late = 2 + chunks // 2 + q // 2
-
-        @pl.when(inner & (q % 2 == 1) & (late < chunks))
-        def _():
-            near_copy(0, late).start()
+        pl.when(inner & (q % 2 == 1))(lambda: near_nth(3 + chunks // 2 + q // 2))
 
     middle = chunks // 2 + 1
     with jax.named_scope("enter_a"):
@@ -614,13 +680,10 @@
         @pl.loop(middle, chunks)
         def _(q):
             enter(1, q)
-            late = 2 + chunks // 2 + q // 2
-
-            @pl.when(inner & (q % 2 == 1) & (late < chunks))
-            def _():
-                near_copy(0, late).start()
-
-        pl.when(inner)(lambda: each(lambda q: near_copy(1, q).start()))
+
+        @pl.when(inner)
+        def _():
+            pl.loop(3 + chunks // 2 + middle // 2, 2 * chunks)(near_nth)
 
     loads[2].wait()
     with jax.named_scope("contract_b"):
@@ -634,29 +697,31 @@
 
         gathered(3)
     with jax.named_scope("expand_a"):
-        expand(3, 1)
+        expand(3, 1, (early(2, 0),))
+    def spread_near(q):
+        @pl.when(q == chunks - 1)
+        def _():
+            for k, r in ((0, row), (1, 1 - row)):
+                slot = r * 2 + core
+                remote(near_stage.at[k], x.at[near_j, slot], near_send.at[k], near_recv.at[k], near).wait_recv()
+                d_whole(near_j, r, core).start()
+
     with jax.named_scope("contract_a"):
-        contract(3, 1, 1, False, (finish(2, 0), lagged(0)))
+        contract(3, 1, 1, False, (ahead(2, 0), merge_most(0), spread_near))
         release()
-    with jax.named_scope("merge_b"):
-        merge_rest(0)
 
     with jax.named_scope("wait_near"):
-        for k, r in ((0, row), (1, 1 - row)):
-            slot = r * 2 + core
-            remote(near_stage.at[k], x.at[near_j, slot], near_send.at[k], near_recv.at[k], near).wait_recv()
-            d_whole(near_j, r, core).start()
-
         gathered(near_j)
     with jax.named_scope("expand_near"):
-        expand(near_j, 1)
+        expand(near_j, 1, (early(3, 1),))
     with jax.named_scope("contract_near"):
-        contract(near_j, 0, 1, True, (finish(3, 1), lagged(1)))
+        contract(near_j, 0, 1, True, (merge_last(0), ahead(3, 1), merge_most(1)))
         release()
-    with jax.named_scope("merge_a"):
-        merge_rest(1)
+    def merge_late(q):
+        pl.when(q >= chunks - 2)(lambda: merge(1)(q))
+
     with jax.named_scope("contract_own"):
-        contract(own_j, 1, 0, True, (finish(near_j, 0),))
+        contract(own_j, 1, 0, True, (finish(near_j, 0), merge_late))
 
     with jax.named_scope("combine"):
         remote(raw, raw_y, cross_send, cross_recv.at[0], neighbour).wait_send()
@@ -672,7 +737,19 @@
             with jax.named_scope("w_fr"):
                 fr_copy(0, q).wait_recv()
             total = mixed(0, x[own_j, s, :, cols], near_ret[:, cols])
-            raw[:, cols] = (total + far_ret[:, cols].astype(jnp.float32)).astype(raw.dtype)
+            total += far_ret[:, cols].astype(jnp.float32)
+
+            @pl.when(~folded(q))
+            def _():
+                raw[:, cols] = total.astype(raw.dtype)
+
+            @pl.when(folded(q))
+            def _():
+                with jax.named_scope("w_fin"):
+                    fin_copy(q).wait_recv()
+                rest = raw_y[:, columns((q + folds) % chunks)]
+                raw[:, cols] = (total + rest.astype(jnp.float32)).astype(raw.dtype)
+
             out_copy(q).start()
 
     with jax.named_scope("tail_sends"):
@@ -682,7 +759,11 @@
         sent(x.at[near_j, s], near_ret, nr_send)
         for j in range(4):
             sent(x.at[j, pl.ds(0, 2)], pair.at[0], rp_send.at[j])
-            sent(x.at[j, cross_s], near_ret, ry_send.at[j])
+            part = pl.ds(0, width if j >= 2 else width - folds * tile)
+            sent(x.at[j, cross_s, :, part], near_ret.at[:, part], ry_send.at[j])
+        sent(near_cross, near_cross, nx_send)
+        part = pl.ds(0, folds * tile)
+        sent(raw_y.at[:, part], far_ret.at[:, part], fin_send)
 
         @pl.when(inner)
         def _():
@@ -703,6 +784,7 @@
     tok_rows, width = tokens.shape
     ff, dtype = w_gate.shape[2], tokens.dtype
     rows, chunks = SHARDS * cap, width // tile_of(width, 1024)
+    folds = chunks * 3 // 7
     dma, vmem = pltpu.SemaphoreType.DMA, pltpu.VMEM
     anywhere, local = pl.BlockSpec(memory_space=pl.ANY), pl.BlockSpec(memory_space=pltpu.VMEM)
     return pl.pallas_call(
@@ -724,11 +806,12 @@
             vmem((2, tok_rows, width), dtype),
             vmem((2, cap, width), dtype),
             vmem((cap, width), dtype),
+            vmem((folds, cap, width // chunks), dtype),
             vmem((2, cap, width), dtype),
             vmem((tok_rows, width), dtype),
             vmem((4, 16, tok_rows), jnp.float32),
             vmem((4, 2 * cap, tok_rows), dtype),
-            vmem((3, 2, tok_rows, 2 * cap), dtype),
+            vmem((4, 2, tok_rows, 2 * cap), dtype),
             dma((3,)), dma, dma, dma((2,)), dma((3,)),
             dma, dma((chunks,)), dma, dma((2, chunks)),
             dma((2,)), dma((2,)),
@@ -740,6 +823,7 @@
             dma, dma((chunks,)),
             dma((2,)), dma((2, chunks)),
             dma((2,)), dma((chunks,)),
+            dma, dma((folds,)), dma, dma((folds,)),
             pltpu.SemaphoreType.REGULAR, pltpu.SemaphoreType.REGULAR,
         ],
         compiler_params=pltpu.CompilerParams(

time: 202 us -> 198 us (0.980)
  Pallas kernels: 198 us -> 194 us
    pallas_call x1, Pallas kernels: 198 us -> 194 us  [routed(): pl.pallas_call(routed_kernel, out_shape=jax.ShapeDtypeStruct((tok_rows, w...]
where the time goes in v4:
time: 198 us; the launch traced here: 197 us
  Pallas kernels  194 us (98%)
  local copies, waits for them, and re-layouts  2.85 us (1%)
    pallas_call x1, Pallas kernels, routed(): pl.pallas_call(routed_kernel, out_shape=jax.ShapeDtypeStruct((tok_rows, w...  194 us

profile of v4, /device:TPU:0, one launch (start us, length us, event | category | flops | bytes accessed | tf_op | source)
XLA Modules:
  0.0 196.6 jit_solution(3825763538828932915)
XLA Ops:
  0.0 193.8 %shard_map.64 = bf16[128,7168]{1,0:T(8,128)(2,1)} custom-call(bf16[128,7168]{1,0:T(8,128)(2,1)} %tokens.1, s32[2,128]{1,0:T(2,128)} %bitcast.2, s32[2,128]{1,0:T(2,128)} %bitcast.3, bf16[1,7168,512]{2,1,0:T(8,128)(2,1)} %gate_hbm.1, bf16[1,7168,512]{2,1,0:T(8,128)(2,1)} %up_hbm.1, bf16[1,512,7168]{2,1,0:T(8,128)(2,1)} %down_hbm.1), custom_call_target="tpu_custom_call" | custom-call | tf_op jit(solution)/shard_map/pallas_call | solution.py:790
  193.8 2.8 %copy.8 = bf16[128,7168]{1,0:T(8,128)(2,1)} copy(bf16[128,7168]{1,0:T(8,128)(2,1)} %shard_map.64) | data formatting | bytes 3670016

commit v5 on v4

--- a/solution.py
+++ b/solution.py
@@ -219,10 +219,10 @@
 
 
 def routed_kernel(
-    tokens, ids, levels, gate_hbm, up_hbm, down_hbm, out_hbm,
+    tokens, ids, levels, gate_hbm, up_hbm, down_hbm, far_ret,
     x, gate, up, down, acc, hidden, pair, cross, raw, raw_y, raw_f,
-    near_stage, near_ret, near_cross, outer_ret, far_ret, table, picks, mix,
-    w_sem, raw_sem, out_sem, table_send, table_recv,
+    near_stage, near_ret, near_cross, outer_ret, table, picks, mix,
+    w_sem, raw_sem, table_send, table_recv,
     cross_send, cross_recv, far_send, far_recv, near_send, near_recv,
     fwd_send, fwd_recv, y_send, y_recv, d_send, d_recv,
     rp_send, rp_recv, ry_send, ry_recv,
@@ -412,10 +412,6 @@
             far_b if i == 0 else far,
         )
 
-    def out_copy(q):
-        cols = columns(q)
-        return pltpu.make_async_copy(raw.at[:, cols], out_hbm.at[:, cols], out_sem)
-
     def folded(q):
         return (q >= 2) & (q < 2 + folds)
 
@@ -426,7 +422,7 @@
 
     def fin_copy(q):
         return remote(
-            raw_y.at[:, columns(q)], raw_y.at[:, columns((q + folds) % chunks)],
+            raw.at[:, columns(q)], raw_y.at[:, columns(q)],
             fin_send, fin_recv.at[q - 2], neighbour,
         )
 
@@ -435,7 +431,7 @@
         with jax.named_scope("w_nx"):
             nx_copy(q).wait_recv()
         total = mixed(3, x[own_j, cross_s, :, cols], near_cross[q - 2])
-        raw_y[:, cols] = total.astype(raw_y.dtype)
+        raw[:, cols] = total.astype(raw.dtype)
         fin_copy(q).start()
 
     def expand(j, spot, also=()):
@@ -538,7 +534,8 @@
                 @pl.when(q == 0)
                 def _():
                     sent(raw_f.at[i, pl.ds(0, cap)], near_ret, fwd_send.at[i])
-                    if i == 0:
+                    with jax.named_scope("w_gate"):
+                      if i == 0:
                         sent(near_stage.at[1], near_ret, near_send.at[1])
 
                 with jax.named_scope("w_or"):
@@ -648,6 +645,7 @@
             pl.when(inner & (q % 2 == 1))(lambda: near_copy(0, 2 + q // 2).start())
 
     pl.when(inner)(lambda: near_nth(2 + chunks // 2))
+    pl.when(inner)(lambda: near_nth(3 + chunks // 2))
 
     with jax.named_scope("wait_own"):
         loads[0].wait()
@@ -660,7 +658,7 @@
         enter(1, q)
         y_arrival(0, q).wait_recv()
         d_copy(2, 1 - row, q).start()
-        pl.when(inner & (q % 2 == 1))(lambda: near_nth(3 + chunks // 2 + q // 2))
+        pl.when(inner & (q % 2 == 1))(lambda: near_nth(4 + chunks // 2 + q // 2))
 
     middle = chunks // 2 + 1
     with jax.named_scope("enter_a"):
@@ -683,7 +681,7 @@
 
         @pl.when(inner)
         def _():
-            pl.loop(3 + chunks // 2 + middle // 2, 2 * chunks)(near_nth)
+            pl.loop(4 + chunks // 2 + middle // 2, 2 * chunks)(near_nth)
 
     loads[2].wait()
     with jax.named_scope("contract_b"):
@@ -720,13 +718,12 @@
     def merge_late(q):
         pl.when(q >= chunks - 2)(lambda: merge(1)(q))
 
+    sent(raw, raw_y, cross_send)
+    sent(raw, raw_y, far_send)
     with jax.named_scope("contract_own"):
         contract(own_j, 1, 0, True, (finish(near_j, 0), merge_late))
 
     with jax.named_scope("combine"):
-        remote(raw, raw_y, cross_send, cross_recv.at[0], neighbour).wait_send()
-        remote(raw, raw_y, far_send, cross_recv.at[0], neighbour).wait_send()
-
         @each
         def _(q):
             cols = columns(q)
@@ -741,16 +738,15 @@
 
             @pl.when(~folded(q))
             def _():
-                raw[:, cols] = total.astype(raw.dtype)
+                far_ret[:, cols] = total.astype(far_ret.dtype)
 
             @pl.when(folded(q))
             def _():
                 with jax.named_scope("w_fin"):
                     fin_copy(q).wait_recv()
-                rest = raw_y[:, columns((q + folds) % chunks)]
-                raw[:, cols] = (total + rest.astype(jnp.float32)).astype(raw.dtype)
-
-            out_copy(q).start()
+                rest = raw_y[:, cols].astype(jnp.float32)
+                far_ret[:, cols] = (total + rest).astype(far_ret.dtype)
+
 
     with jax.named_scope("tail_sends"):
         table_y.wait_send()
@@ -763,7 +759,7 @@
             sent(x.at[j, cross_s, :, part], near_ret.at[:, part], ry_send.at[j])
         sent(near_cross, near_cross, nx_send)
         part = pl.ds(0, folds * tile)
-        sent(raw_y.at[:, part], far_ret.at[:, part], fin_send)
+        sent(raw.at[:, part], far_ret.at[:, part], fin_send)
 
         @pl.when(inner)
         def _():
@@ -775,9 +771,6 @@
             sent(near_stage.at[1], near_ret, near_send.at[1])
             for i in range(2):
                 sent(x.at[2 + i, s], near_ret, or_send.at[i])
-
-    with jax.named_scope("tail_out"):
-        pltpu.make_async_copy(raw, out_hbm, out_sem).wait()
 
 
 def routed(tokens, route_ids, levels, w_gate, w_up, w_down, cap):
@@ -789,9 +782,9 @@
     anywhere, local = pl.BlockSpec(memory_space=pl.ANY), pl.BlockSpec(memory_space=pltpu.VMEM)
     return pl.pallas_call(
         routed_kernel,
-        out_shape=jax.ShapeDtypeStruct((tok_rows, width), dtype),
+        out_shape=pltpu.VMEM((tok_rows, width), dtype),
         in_specs=[anywhere, local, local, anywhere, anywhere, anywhere],
-        out_specs=anywhere,
+        out_specs=local,
         scratch_shapes=[
             vmem((4, SHARDS, cap, width), dtype),
             vmem((width, ff), dtype),
@@ -808,11 +801,10 @@
             vmem((cap, width), dtype),
             vmem((folds, cap, width // chunks), dtype),
             vmem((2, cap, width), dtype),
-            vmem((tok_rows, width), dtype),
             vmem((4, 16, tok_rows), jnp.float32),
             vmem((4, 2 * cap, tok_rows), dtype),
             vmem((4, 2, tok_rows, 2 * cap), dtype),
-            dma((3,)), dma, dma, dma((2,)), dma((3,)),
+            dma((3,)), dma, dma((2,)), dma((3,)),
             dma, dma((chunks,)), dma, dma((2, chunks)),
             dma((2,)), dma((2,)),
             dma((2,)), dma((2, chunks)),
@@ -827,7 +819,7 @@
             pltpu.SemaphoreType.REGULAR, pltpu.SemaphoreType.REGULAR,
         ],
         compiler_params=pltpu.CompilerParams(
-            collective_id=0, has_side_effects=True, vmem_limit_bytes=67_000_000
+            collective_id=0, has_side_effects=True, vmem_limit_bytes=65_200_000
         ),
     )(tokens, route_ids.T, levels.T, w_gate, w_up, w_down)
 

time: 198 us -> 196 us (0.990)
  no operation moved by 1% of the time
where the time goes in v5:
time: 196 us
  Pallas kernels  194 us (99%)
    pallas_call x1, Pallas kernels, routed(): pl.pallas_call(routed_kernel, out_shape=pltpu.VMEM((tok_rows, width), dty...  194 us

profile of v5, /device:TPU:0, one launch (start us, length us, event | category | flops | bytes accessed | tf_op | source)
XLA Modules:
  0.0 195.5 jit_solution(10571148841206946261)
XLA Ops:
  0.0 194.3 %shard_map.64 = bf16[128,7168]{1,0:T(8,128)(2,1)S(1)} custom-call(bf16[128,7168]{1,0:T(8,128)(2,1)} %tokens.1, s32[2,128]{1,0:T(2,128)} %bitcast.2, s32[2,128]{1,0:T(2,128)} %bitcast.3, bf16[1,7168,512]{2,1,0:T(8,128)(2,1)} %gate_hbm.1, bf16[1,7168,512]{2,1,0:T(8,128)(2,1)} %up_hbm.1, bf16[1,512,7168]{2,1,0:T(8,128)(2,1)} %down_hbm.1), custom_call_target="tpu_custom_call" | custom-call | tf_op jit(solution)/shard_map/pallas_call | solution.py:783
  194.3 1.2 copy.8

commit v6 on v5

--- a/solution.py
+++ b/solution.py
@@ -228,7 +228,7 @@
     rp_send, rp_recv, ry_send, ry_recv,
     nr_send, nr_recv, or_send, or_recv, fr_send, fr_recv,
     nx_send, nx_recv, fin_send, fin_recv,
-    pair_free, cross_free,
+    pair_free, cross_free, entered,
 ):
     me = lax.axis_index("expert")
     plane, s = me // SHARDS, me % SHARDS
@@ -272,13 +272,13 @@
     raw_load.start()
 
     barrier = pltpu.get_barrier_semaphore()
-    peers = [partner, neighbour, near, far]
+    peers = [partner, neighbour, near]
     for peer in peers:
         pl.semaphore_signal(barrier, inc=1, device_id={"expert": peer}, device_id_type=MESH)
 
     @pl.when(inner)
     def _():
-        pl.semaphore_signal(barrier, inc=1, device_id={"expert": far_b}, device_id_type=MESH)
+        pl.semaphore_signal(barrier, inc=1, device_id={"expert": far}, device_id_type=MESH)
 
     lane = lax.broadcasted_iota(jnp.int32, (tok_rows, tok_rows), 1)
     line = lax.broadcasted_iota(jnp.int32, (tok_rows, tok_rows), 0)
@@ -328,7 +328,11 @@
     table_y = remote(table.at[0], table.at[1], table_send.at[0], table_recv.at[0], neighbour)
     table_f = remote(table.at[0], table.at[3 - kind], table_send.at[1], table_recv.at[2 - kind], far)
     table_y.start()
-    table_f.start()
+
+    @pl.when(inner)
+    def _():
+        for peer in (near, far):
+            pl.semaphore_signal(entered, inc=1, device_id={"expert": peer}, device_id_type=MESH)
 
     def table_arrival(k):
         return remote(table.at[0], table.at[k], table_send.at[0], table_recv.at[k - 1], far)
@@ -548,8 +552,8 @@
 
     def early(j, t):
         def step(q):
-            pl.when(q == chunks // 2)(lambda: finish(j, t)(0))
-            pl.when(q == chunks - 1)(lambda: finish(j, t)(1))
+            pl.when(q == chunks // 2 - kind)(lambda: finish(j, t)(0))
+            pl.when(q == chunks - 1 - kind)(lambda: finish(j, t)(1))
 
         return step
 
@@ -605,6 +609,8 @@
     with jax.named_scope("w_raw"):
         raw_load.wait()
     each(lambda q: cross_copy(q).start())
+    pl.when(outer)(lambda: pl.semaphore_wait(entered, 1))
+    table_f.start()
     each(lambda q: far_copy(q, 1 - kind).start())
     for load in loads:
         load.start()
@@ -623,6 +629,7 @@
                 near_copy(0, q).start()
 
     with jax.named_scope("tables"):
+        pl.when(inner)(lambda: pl.semaphore_wait(entered, 1))
         table_arrival(1).wait_recv()
         set_pick(1)
         set_mix(1, 3)
@@ -684,15 +691,14 @@
             pl.loop(4 + chunks // 2 + middle // 2, 2 * chunks)(near_nth)
 
     loads[2].wait()
+    def spread_a(q):
+        y_arrival(1, q).wait_recv()
+        d_copy(3, 1 - row, q).start()
+
     with jax.named_scope("contract_b"):
-        contract(2, 0, 1, False, ())
+        contract(2, 0, 1, False, (spread_a,))
 
     with jax.named_scope("wait_a"):
-        @each
-        def _(q):
-            y_arrival(1, q).wait_recv()
-            d_copy(3, 1 - row, q).start()
-
         gathered(3)
     with jax.named_scope("expand_a"):
         expand(3, 1, (early(2, 0),))
@@ -817,6 +823,7 @@
             dma((2,)), dma((chunks,)),
             dma, dma((folds,)), dma, dma((folds,)),
             pltpu.SemaphoreType.REGULAR, pltpu.SemaphoreType.REGULAR,
+            pltpu.SemaphoreType.REGULAR,
         ],
         compiler_params=pltpu.CompilerParams(
             collective_id=0, has_side_effects=True, vmem_limit_bytes=65_200_000

time: 196 us -> 196 us (level)
  no operation moved by 1% of the time
where the time goes in v6:
time: 196 us
  Pallas kernels  194 us (99%)
    pallas_call x1, Pallas kernels, routed(): pl.pallas_call(routed_kernel, out_shape=pltpu.VMEM((tok_rows, width), dty...  194 us

profile of v6, /device:TPU:0, one launch (start us, length us, event | category | flops | bytes accessed | tf_op | source)
XLA Modules:
  0.0 195.7 jit_solution(12776680014984934328)
XLA Ops:
  0.0 194.5 %shard_map.64 = bf16[128,7168]{1,0:T(8,128)(2,1)S(1)} custom-call(bf16[128,7168]{1,0:T(8,128)(2,1)} %tokens.1, s32[2,128]{1,0:T(2,128)} %bitcast.2, s32[2,128]{1,0:T(2,128)} %bitcast.3, bf16[1,7168,512]{2,1,0:T(8,128)(2,1)} %gate_hbm.1, bf16[1,7168,512]{2,1,0:T(8,128)(2,1)} %up_hbm.1, bf16[1,512,7168]{2,1,0:T(8,128)(2,1)} %down_hbm.1), custom_call_target="tpu_custom_call" | custom-call | tf_op jit(solution)/shard_map/pallas_call | solution.py:789
  194.5 1.2 copy.8

commit v7 on v6

--- a/solution.py
+++ b/solution.py
@@ -539,8 +539,8 @@
                 def _():
                     sent(raw_f.at[i, pl.ds(0, cap)], near_ret, fwd_send.at[i])
                     with jax.named_scope("w_gate"):
-                      if i == 0:
-                        sent(near_stage.at[1], near_ret, near_send.at[1])
+                        if i == 0:
+                            sent(near_stage.at[1], near_ret, near_send.at[1])
 
                 with jax.named_scope("w_or"):
                     or_copy(i, q).wait_recv()
@@ -624,7 +624,7 @@
             x[own_j, s, :, cols] = taken[:cap]
             d_copy(own_j, row, q).start()
 
-            @pl.when(outer | (q < 2))
+            @pl.when(outer | (q < 4))
             def _():
                 near_copy(0, q).start()
 
@@ -649,10 +649,8 @@
             enter(0, q)
 
             pl.when(outer)(lambda: near_copy(1, q).start())
-            pl.when(inner & (q % 2 == 1))(lambda: near_copy(0, 2 + q // 2).start())
-
-    pl.when(inner)(lambda: near_nth(2 + chunks // 2))
-    pl.when(inner)(lambda: near_nth(3 + chunks // 2))
+            pl.when(inner & (q % 2 == 1))(lambda: near_copy(0, 4 + q // 2).start())
+
 
     with jax.named_scope("wait_own"):
         loads[0].wait()

time: 196 us -> 194 us (0.990)
  no operation moved by 1% of the time
where the time goes in v7:
time: 194 us
  Pallas kernels  193 us (99%)
    pallas_call x1, Pallas kernels, routed(): pl.pallas_call(routed_kernel, out_shape=pltpu.VMEM((tok_rows, width), dty...  193 us

profile of v7, /device:TPU:0, one launch (start us, length us, event | category | flops | bytes accessed | tf_op | source)
XLA Modules:
  0.0 193.9 jit_solution(8303356907512146135)
XLA Ops:
  0.0 192.7 %shard_map.64 = bf16[128,7168]{1,0:T(8,128)(2,1)S(1)} custom-call(bf16[128,7168]{1,0:T(8,128)(2,1)} %tokens.1, s32[2,128]{1,0:T(2,128)} %bitcast.2, s32[2,128]{1,0:T(2,128)} %bitcast.3, bf16[1,7168,512]{2,1,0:T(8,128)(2,1)} %gate_hbm.1, bf16[1,7168,512]{2,1,0:T(8,128)(2,1)} %up_hbm.1, bf16[1,512,7168]{2,1,0:T(8,128)(2,1)} %down_hbm.1), custom_call_target="tpu_custom_call" | custom-call | tf_op jit(solution)/shard_map/pallas_call | solution.py:787
  192.7 1.2 copy.8
